TPU v7x, 32 devices: a whole 2x2x4 slice. The times are simulated.
32 devices in a mesh: shard: 8 (over z, y), width: 4 (over x, core).
Axes of the slice: x: 2, y: 2, z: 4, core: 2. Of those that a mesh axis runs over, the one named last changes fastest.
Arguments:
- weight_gate: float32 [2048, 8192], P('shard', 'width'), may hold values from -0.1875 to 0.1875
- moment_gate: float32 [2048, 8192], P('shard', 'width'), may hold values from -6 to 6
- square_gate: float32 [2048, 8192], P('shard', 'width'), may hold values from 0.1 to 10
- weight_up: float32 [2048, 8192], P('shard', 'width'), may hold values from -0.1875 to 0.1875
- moment_up: float32 [2048, 8192], P('shard', 'width'), may hold values from -6 to 6
- square_up: float32 [2048, 8192], P('shard', 'width'), may hold values from 0.1 to 10
- norm_train: float32 [2048], P(('shard', 'width')), may hold values from 0.25 to 1.75
- norm_step: float32 [2048], P(('shard', 'width')), may hold values from -0.3 to 0.3
Outputs:
- serving_gate: bfloat16 [2048, 8192], P(None, 'width')
- serving_up: bfloat16 [2048, 8192], P(None, 'width')
- scale_gate: float32 [8192], P('width')
- scale_up: float32 [8192], P('width')
- serve_norm: bfloat16 [2048], replicated
- whole_gate: float32 [2048, 8192], P('shard', 'width')
- whole_up: float32 [2048, 8192], P('shard', 'width')
All inputs are finite; a program needn't handle non-finite values. Where the computation divides by a largest or mean magnitude, that divisor is 1e-20 or more.
Results may differ from a plain program's by a relative error of at most 0.001.
Values may be sent and summed in bfloat16 or wider, within the bound.
A program may use at most 128 MiB of HBM per device.

v0:
```python
import functools
import math

import jax
import jax.numpy as jnp
from jax import lax
from jax.experimental import pallas as pl
from jax.experimental.pallas import tpu as pltpu
from jax.sharding import PartitionSpec as P

MESH = pl.DeviceIdType.MESH
learn_rate = 0.02
decay_rate = 0.1
tiny_value = 1e-08
UNIT = 16
MOST = 9


def gather_kernel(
    n, width, layers, group, rows, late_rows, a_count, k_count,
    wg, wu, mx, piece, out, scale_ref, nb,
    wbuf, narrow, maxbuf, in_sem, own_sem, ms, mr, ns1, nr1, ns2, nr2, np_sem, zs, os, ys, rs,
):
    s, w = lax.axis_index("shard"), lax.axis_index("width")
    z, g = s // group, lax.rem(s, group)
    held = wg.shape[0]
    loads = [
        pltpu.make_async_copy(ref, wbuf.at[pl.ds(i * held, held)], in_sem.at[i]) for i, ref in enumerate((wg, wu))
    ]
    for load in loads:
        load.start()
    barrier = pltpu.get_barrier_semaphore()
    for j in range(1, n):
        pl.semaphore_signal(barrier, inc=1, device_id=(lax.rem(s + j, n), w), device_id_type=MESH)
    for j in range(1, width):
        pl.semaphore_signal(barrier, inc=1, device_id=(s, lax.rem(w + j, width)), device_id_type=MESH)
    pl.semaphore_wait(barrier, n - 1 + width - 1)

    def max_copy(j):
        return pltpu.make_async_remote_copy(
            mx, maxbuf.at[s], ms.at[j], mr.at[j], device_id=(lax.rem(s + j, n), w), device_id_type=MESH
        )

    def piece_copy(j):
        return pltpu.make_async_remote_copy(
            piece, nb.at[s, w], ns1.at[j], nr1.at[j], device_id=(s, lax.rem(w + j, width)), device_id_type=MESH
        )

    def norm_copy(j):
        return pltpu.make_async_remote_copy(
            nb.at[s], nb.at[s], ns2.at[j], nr2.at[j], device_id=(lax.rem(s + j, n), w), device_id_type=MESH
        )

    for j in range(1, n):
        max_copy(j).start()
    own_piece = pltpu.make_async_copy(piece, nb.at[s, w], np_sem.at[0])
    own_piece.start()
    for j in range(1, width):
        piece_copy(j).start()

    def span(k):
        if isinstance(k, tuple):
            return pl.ds(pl.multiple_of(a_count * rows + k[0] * late_rows, UNIT), late_rows)
        return pl.ds(pl.multiple_of(k * rows, UNIT), rows)

    def slot(k):
        return a_count + k[0] if isinstance(k, tuple) else k

    def place(source, k):
        return out.at[source, span(k)]

    def own(k):
        return narrow.at[span(k)]

    def copy(src, source, k, sem, device):
        return pltpu.make_async_remote_copy(
            src, place(source, k), sem, rs.at[source, slot(k)], device_id=(device, w), device_id_type=MESH
        )

    def partner(j):
        return z * group + lax.rem(g + j, group)

    def up(src, source, k, sem):
        return copy(src, source, k, sem.at[source, slot(k)], lax.rem(s + group, n))

    def down(src, source, k, sem):
        return copy(src, source, k, sem.at[source, slot(k)], lax.rem(s + n - group, n))

    def across(src, source, k, j):
        return copy(src, source, k, ys.at[j - 1, source, slot(k)], partner(j))

    def arrived(source, k):
        pltpu.make_async_copy(place(source, k), place(source, k), rs.at[source, slot(k)]).wait()

    for load in loads:
        load.wait()
    for j in range(1, n):
        max_copy(j).wait_recv()
    scale = mx[...]
    for j in range(1, n):
        scale = jnp.maximum(scale, maxbuf[lax.rem(s + n - j, n)])
    scale_ref[...] = scale

    def own_copy(k):
        return pltpu.make_async_copy(own(k), place(s, k), own_sem.at[slot(k)])

    def divide(unit):
        at = pl.ds(pl.multiple_of(unit * UNIT, UNIT), UNIT)
        scaled = wbuf[at, :] / scale_ref[pl.ds(unit * UNIT // held, 1), :]
        narrow[at, :] = scaled.astype(narrow.dtype)

    @pl.loop(0, a_count)
    def _(k):
        @pl.loop(0, rows // UNIT)
        def _(u):
            divide(k * (rows // UNIT) + u)

        @pl.when(z + 1 < layers)
        def _():
            up(own(k), s, k, zs).start()

        @pl.when(z > 0)
        def _():
            down(own(k), s, k, os).start()

        for j in range(1, group):
            across(own(k), s, k, j).start()
        own_copy(k).start()

    @pl.loop(a_count * rows // UNIT, 2 * held // UNIT)
    def _(u):
        divide(u)

    @pl.loop(0, k_count - a_count)
    def _(q):
        k = (q,)
        for j in range(1, group):
            across(own(k), s, k, j).start()
        own_copy(k).start()

    own_piece.wait()
    for j in range(1, width):
        piece_copy(j).wait_recv()
    for j in range(1, n):
        norm_copy(j).start()

    for d in range(1, layers):
        @pl.loop(0, a_count)
        def _(k):
            @pl.when(z - d >= 0)
            def _():
                source = s - d * group
                arrived(source, k)

                @pl.when(z + 1 < layers)
                def _():
                    up(place(source, k), source, k, zs).start()

                for j in range(1, group):
                    across(place(source, k), source, k, j).start()

            @pl.when(z + d < layers)
            def _():
                source = s + d * group
                arrived(source, k)

                @pl.when(z > 0)
                def _():
                    down(place(source, k), source, k, zs).start()

                for j in range(1, group):
                    across(place(source, k), source, k, j).start()

    for j in range(group):
        source = partner(j)

        @pl.loop(0, k_count - a_count)
        def _(q):
            k = (q,)
            if j:
                arrived(source, k)
            src = place(source, k) if j else own(k)

            @pl.when(z + 1 < layers)
            def _():
                up(src, source, k, zs).start()

            @pl.when(z > 0)
            def _():
                down(src, source, k, os).start()

    for d in range(1, layers):
        for j in range(group):
            @pl.loop(0, k_count - a_count)
            def _(q):
                k = (q,)

                @pl.when(z - d >= 0)
                def _():
                    source = partner(j) - d * group
                    arrived(source, k)

                    @pl.when(z + 1 < layers)
                    def _():
                        up(place(source, k), source, k, zs).start()

                @pl.when(z + d < layers)
                def _():
                    source = partner(j) + d * group
                    arrived(source, k)

                    @pl.when(z > 0)
                    def _():
                        down(place(source, k), source, k, zs).start()

    for j in range(1, group):
        @pl.loop(0, layers)
        def _(layer):
            @pl.loop(0, a_count)
            def _(k):
                arrived(layer * group + lax.rem(g + j, group), k)

    def left(source, k, layer):
        @pl.when((layer <= z) & (z + 1 < layers))
        def _():
            up(place(source, k), source, k, zs).wait_send()

        @pl.when((layer > z) & (z > 0))
        def _():
            down(place(source, k), source, k, zs).wait_send()

        @pl.when((layer == z) & (z > 0))
        def _():
            down(place(source, k), source, k, os).wait_send()

    @pl.loop(0, a_count)
    def _(k):
        own_copy(k).wait()

        @pl.loop(0, layers)
        def _(layer):
            source = layer * group + g
            left(source, k, layer)
            for j in range(1, group):
                across(place(source, k), source, k, j).wait_send()

    @pl.loop(0, k_count - a_count)
    def _(q):
        k = (q,)
        own_copy(k).wait()
        for j in range(1, group):
            across(own(k), s, k, j).wait_send()

        @pl.loop(0, layers)
        def _(layer):
            for j in range(group):
                left(layer * group + lax.rem(g + j, group), k, layer)

    for j in range(1, width):
        piece_copy(j).wait_send()
    for j in range(1, n):
        max_copy(j).wait_send()
        norm_copy(j).wait()


def solution(mesh):
    n, width = mesh.shape["shard"], mesh.shape["width"]
    layers = math.gcd(n, math.isqrt(2 * n))
    group = n // layers

    def body(
        weight_gate, moment_gate, square_gate, weight_up, moment_up, square_up, norm_train, norm_step
    ):
        whole_gate = weight_gate - learn_rate * (
            moment_gate / (jnp.sqrt(square_gate) + tiny_value) + decay_rate * weight_gate
        )
        whole_up = weight_up - learn_rate * (
            moment_up / (jnp.sqrt(square_up) + tiny_value) + decay_rate * weight_up
        )
        local = jnp.stack([jnp.max(jnp.abs(whole_gate), axis=0), jnp.max(jnp.abs(whole_up), axis=0)])
        count = norm_train.shape[0]
        lanes = -(-count // 128) * 128
        piece = jnp.pad((norm_train + norm_step)[None, :], ((0, 7), (0, lanes - count)))
        held, columns = whole_gate.shape
        units = 2 * held // UNIT
        late_units = max(1, units * 5 // 32)
        early_units = units - late_units
        step = max(d for d in range(1, MOST + 1) if early_units % d == 0)
        rows, late_rows = step * UNIT, late_units * UNIT
        a_count, k_count = early_units // step, early_units // step + 1
        any_space = pl.BlockSpec(memory_space=pl.ANY)
        vmem_space = pl.BlockSpec(memory_space=pltpu.VMEM)
        dma = pltpu.SemaphoreType.DMA
        out, scale, nb = pl.pallas_call(
            functools.partial(gather_kernel, n, width, layers, group, rows, late_rows, a_count, k_count),
            out_shape=(
                jax.ShapeDtypeStruct((n, 2 * held, columns), jnp.bfloat16),
                jax.ShapeDtypeStruct((2, columns), jnp.float32),
                jax.ShapeDtypeStruct((n, width, 8, lanes), jnp.float32),
            ),
            in_specs=[any_space, any_space, vmem_space, vmem_space],
            out_specs=(any_space, vmem_space, any_space),
            scratch_shapes=[
                pltpu.VMEM((2 * held, columns), jnp.float32),
                pltpu.VMEM((2 * held, columns), jnp.bfloat16),
                pltpu.VMEM((n, 2, columns), jnp.float32),
                dma((2,)),
                dma((k_count,)),
                dma((n,)),
                dma((n,)),
                dma((width,)),
                dma((width,)),
                dma((n,)),
                dma((n,)),
                dma((1,)),
                dma((n, k_count)),
                dma((n, k_count)),
                dma((max(1, group - 1), n, k_count)),
                dma((n, k_count)),
            ],
            compiler_params=pltpu.CompilerParams(
                collective_id=0, has_side_effects=True, vmem_limit_bytes=14 << 20
            ),
            name="gather",
        )(whole_gate, whole_up, local, piece)
        serve_norm = nb[:, :, 0, :count].reshape(-1).astype(jnp.bfloat16)
        return (
            out[:, :held].reshape(n * held, columns),
            out[:, held:].reshape(n * held, columns),
            scale[0],
            scale[1],
            serve_norm,
            whole_gate,
            whole_up,
        )

    return jax.shard_map(
        body,
        mesh=mesh,
        in_specs=(P("shard", "width"),) * 6 + (P(("shard", "width")),) * 2,
        out_specs=(
            P(None, "width"),
            P(None, "width"),
            P("width"),
            P("width"),
            P(),
            P("shard", "width"),
            P("shard", "width"),
        ),
        check_vma=False,
    )
```

profile of v0, /device:TPU:0, one launch (start us, length us, event | category | flops | bytes accessed | tf_op | source)
XLA Modules:
  0.0 188.8 jit_solution(4487426726366271255)
XLA Ops:
  0.6 0.7 add_bitcast_fusion
  1.3 6.7 %abs_reduce_fusion = (f32[2048]{0:T(1024)S(1)}, f32[256,2048]{1,0:T(8,128)S(1)}, f32[2048]{0:T(1024)S(1)}, f32[256,2048]{1,0:T(8,128)S(1)}) fusion(f32[256,2048]{1,0:T(8,128)} %param.11, f32[256,2048]{1,0:T(8,128)} %param.12, f32[256,2048]{1,0:T(8,128)} %param.13, f32[256,2048]{1,0:T(8,128)} %param.8, f32[256,2048]{1,0:T(8,128)} %param.9, f32[256,2048]{1,0:T(8,128)} %param.10), kind=kLoop, calls=%fused_computation | loop fusion | flops 8384512 | bytes 16793600 | tf_op jit(solution)/shard_map/reduce_max | solution.py:280
  8.0 0.0 copy-start
  8.0 0.0 copy-start.1
  8.0 173.0 %gather.1 = (bf16[8,512,2048]{2,1,0:T(8,128)(2,1)S(1)}, f32[2,2048]{1,0:T(2,128)S(1)}, f32[8,4,8,128]{3,2,1,0:T(8,128)S(1)}) custom-call(f32[256,2048]{1,0:T(8,128)S(1)} %get-tuple-element.22.wg, f32[256,2048]{1,0:T(8,128)S(1)} %get-tuple-element.16.wu, f32[2,2048]{1,0:T(2,128)S(1)} %pad_maximum_fusion.mx, f32[8,128]{1,0:T(8,128)S(1)} %pad.4.piece), custom_call_target="tpu_custom_call" | custom-call | tf_op jit(solution)/shard_map/gather/pallas_call | solution.py:294
  181.0 0.0 copy-done
  181.0 0.0 copy-done.1
  181.1 6.4 %fusion.1 = (bf16[8,256,2048]{2,1,0:T(8,128)(2,1)}, bf16[8,256,2048]{2,1,0:T(8,128)(2,1)}) fusion(bf16[8,512,2048]{2,1,0:T(8,128)(2,1)S(1)} %get-tuple-element.10), kind=kLoop, calls=%fused_computation.8 | loop fusion | bytes 33554432 | tf_op jit(solution)/shard_map/slice | solution.py:329
  187.4 0.1 fusion
  187.5 0.7 convert_element_type.6
  188.2 0.6 fusion.2
  (2 shorter events, 0.0 us)
Async XLA Ops:
  8.0 173.0 %copy-start = (f32[256,2048]{1,0:T(8,128)}, f32[256,2048]{1,0:T(8,128)S(1)}, u32[]{:S(2)}) copy-start(f32[256,2048]{1,0:T(8,128)S(1)} %get-tuple-element.16.wu) | copy-start | bytes 6291460
  8.0 173.0 %copy-start.1 = (f32[256,2048]{1,0:T(8,128)}, f32[256,2048]{1,0:T(8,128)S(1)}, u32[]{:S(2)}) copy-start(f32[256,2048]{1,0:T(8,128)S(1)} %get-tuple-element.22.wg) | copy-start | bytes 6291460
where the time goes:
time: 189 us
  Pallas kernels  173 us (92%)
  local copies, waits for them, and re-layouts  7.75 us (4%)
  other arithmetic  7.37 us (4%)
    pallas_call x1, Pallas kernels, body(): pl.pallas_call(functools.partial(gather_kernel, n, width, layers, group,...  173 us
    reduce_max x1, other arithmetic, body(): jnp.max(jnp.abs(whole_up), axis=0)  6.67 us
    slice x1, local copies, waits for them, and re-layouts, body(): out[:, held:].reshape(n * held, columns)  6.39 us

commit v1 on v0

v1 whole, which is shorter than its diff:
```python
import functools
import math

import jax
import jax.numpy as jnp
from jax import lax
from jax.experimental import pallas as pl
from jax.experimental.pallas import tpu as pltpu
from jax.sharding import PartitionSpec as P

MESH = pl.DeviceIdType.MESH
learn_rate = 0.02
decay_rate = 0.1
tiny_value = 1e-08
UNIT = 16
MOST = 9
LOAD = 32
BLOCK = 8
VMEM_LIMIT = 12 << 20


def gather_kernel(
    n, width, layers, group, rows, late_rows, a_count, k_count, count,
    wg, mg, sg, wu, mu, su, train, change,
    out, whole, scale_ref, norm,
    moment, square, mx, maxbuf, inv, terms, pieces, share, shares,
    in_sem, term_sem, ms, mr, ns1, nr1, ns2, nr2, zs, os, ys, rs,
):
    s, w = lax.axis_index("shard"), lax.axis_index("width")
    z, g = s // group, lax.rem(s, group)
    held, columns = wg.shape
    loads = held // LOAD
    parts = ((wg, whole), (mg, moment), (sg, square)), ((wu, whole), (mu, moment), (su, square))

    def load(m, i, c):
        source, target = parts[m][i]
        at = pl.multiple_of(c * LOAD, LOAD)
        return pltpu.make_async_copy(
            source.at[pl.ds(at, LOAD)], target.at[pl.ds(m * held + at, LOAD)], in_sem.at[m, i, c]
        )

    for m in range(2):
        @pl.loop(0, loads)
        def _(c):
            for i in range(3):
                load(m, i, c).start()

    term_loads = [
        pltpu.make_async_copy(ref, terms.at[i], term_sem.at[i]) for i, ref in enumerate((train, change))
    ]
    for term in term_loads:
        term.start()

    barrier = pltpu.get_barrier_semaphore()
    for j in range(1, n):
        pl.semaphore_signal(barrier, inc=1, device_id=(lax.rem(s + j, n), w), device_id_type=MESH)
    for j in range(1, width):
        pl.semaphore_signal(barrier, inc=1, device_id=(s, lax.rem(w + j, width)), device_id_type=MESH)

    def max_copy(m, j):
        return pltpu.make_async_remote_copy(
            mx.at[m], maxbuf.at[m, s], ms.at[m, j], mr.at[m, j],
            device_id=(lax.rem(s + j, n), w), device_id_type=MESH,
        )

    def piece_copy(j):
        return pltpu.make_async_remote_copy(
            pieces.at[w], pieces.at[w], ns1.at[j], nr1.at[j],
            device_id=(s, lax.rem(w + j, width)), device_id_type=MESH,
        )

    def norm_copy(j):
        return pltpu.make_async_remote_copy(
            shares.at[s], shares.at[s], ns2.at[j], nr2.at[j],
            device_id=(lax.rem(s + j, n), w), device_id_type=MESH,
        )

    def update(m):
        def chunk(c, top):
            for i in range(3):
                load(m, i, c).wait()

            def block(b, top):
                at = pl.ds(pl.multiple_of(m * held + c * LOAD + b * BLOCK, BLOCK), BLOCK)
                old = whole[at, :]
                new = old - learn_rate * (moment[at, :] / (jnp.sqrt(square[at, :]) + tiny_value) + decay_rate * old)
                whole[at, :] = new
                return jnp.maximum(top, jnp.abs(new))

            return lax.fori_loop(0, LOAD // BLOCK, block, top)

        top = lax.fori_loop(0, loads, chunk, jnp.zeros((BLOCK, columns), jnp.float32))
        mx[m] = jnp.max(top, axis=0, keepdims=True)

    def scale(m):
        for j in range(1, n):
            max_copy(m, j).wait_recv()
        top = mx[m]
        for j in range(1, n):
            top = jnp.maximum(top, maxbuf[m, lax.rem(s + n - j, n)])
        scale_ref[m] = top
        inv[m] = 1.0 / top

    update(0)
    lane = lax.broadcasted_iota(jnp.int32, (1, 128), 1)
    per = 128 // count
    spot = lax.rem(s * width + w, per)
    for term in term_loads:
        term.wait()
    piece = jnp.concatenate([terms[0] + terms[1]] * per, axis=1)
    pieces[w] = jnp.where(lane // count == spot, piece, 0.0)
    pl.semaphore_wait(barrier, n - 1 + width - 1)
    for j in range(1, n):
        max_copy(0, j).start()
    for j in range(1, width):
        piece_copy(j).start()
    update(1)
    for j in range(1, n):
        max_copy(1, j).start()
    for j in range(1, width):
        piece_copy(j).wait_recv()
    lines = max(1, width // per)
    for r in range(lines):
        total = pieces[r * (width // lines)]
        for i in range(1, width // lines):
            total = total + pieces[r * (width // lines) + i]
        share[r] = total
        shares[s, r] = total
    for j in range(1, n):
        norm_copy(j).start()

    def span(k):
        if isinstance(k, tuple):
            return pl.ds(pl.multiple_of(a_count * rows + k[0] * late_rows, UNIT), late_rows)
        return pl.ds(pl.multiple_of(k * rows, UNIT), rows)

    def slot(k):
        return a_count + k[0] if isinstance(k, tuple) else k

    def place(source, k):
        return out.at[source, span(k)]

    def copy(source, k, sem, device):
        return pltpu.make_async_remote_copy(
            place(source, k), place(source, k), sem, rs.at[source, slot(k)], device_id=(device, w), device_id_type=MESH
        )

    def partner(j):
        return z * group + lax.rem(g + j, group)

    def up(source, k, sem):
        return copy(source, k, sem.at[source, slot(k)], lax.rem(s + group, n))

    def down(source, k, sem):
        return copy(source, k, sem.at[source, slot(k)], lax.rem(s + n - group, n))

    def across(source, k, j):
        return copy(source, k, ys.at[j - 1, source, slot(k)], partner(j))

    def arrived(source, k):
        pltpu.make_async_copy(place(source, k), place(source, k), rs.at[source, slot(k)]).wait()

    def divide(m, unit):
        at = pl.ds(pl.multiple_of(unit * UNIT, UNIT), UNIT)
        out[s, at, :] = (whole[at, :] * inv[m]).astype(out.dtype)

    per_matrix = held // UNIT
    done = 0
    scale(0)

    def divide_to(limit):
        nonlocal done
        for m in range(2):
            first, last = max(done, m * per_matrix), min(limit, (m + 1) * per_matrix)
            if first < last:
                if m == 1 and done <= per_matrix:
                    scale(1)

                @pl.loop(first, last)
                def _(u):
                    divide(m, u)

                done = last

    for k in range(a_count):
        divide_to((k + 1) * rows // UNIT)

        @pl.when(z + 1 < layers)
        def _():
            up(s, k, zs).start()

        @pl.when(z > 0)
        def _():
            down(s, k, os).start()

        for j in range(1, group):
            across(s, k, j).start()

    divide_to(2 * held // UNIT)

    @pl.loop(0, k_count - a_count)
    def _(q):
        k = (q,)
        for j in range(1, group):
            across(s, k, j).start()

    for d in range(1, layers):
        @pl.loop(0, a_count)
        def _(k):
            @pl.when(z - d >= 0)
            def _():
                source = s - d * group
                arrived(source, k)

                @pl.when(z + 1 < layers)
                def _():
                    up(source, k, zs).start()

                for j in range(1, group):
                    across(source, k, j).start()

            @pl.when(z + d < layers)
            def _():
                source = s + d * group
                arrived(source, k)

                @pl.when(z > 0)
                def _():
                    down(source, k, zs).start()

                for j in range(1, group):
                    across(source, k, j).start()

    for j in range(group):
        source = partner(j)

        @pl.loop(0, k_count - a_count)
        def _(q):
            k = (q,)
            if j:
                arrived(source, k)

            @pl.when(z + 1 < layers)
            def _():
                up(source, k, zs).start()

            @pl.when(z > 0)
            def _():
                down(source, k, os).start()

    for d in range(1, layers):
        for j in range(group):
            @pl.loop(0, k_count - a_count)
            def _(q):
                k = (q,)

                @pl.when(z - d >= 0)
                def _():
                    source = partner(j) - d * group
                    arrived(source, k)

                    @pl.when(z + 1 < layers)
                    def _():
                        up(source, k, zs).start()

                @pl.when(z + d < layers)
                def _():
                    source = partner(j) + d * group
                    arrived(source, k)

                    @pl.when(z > 0)
                    def _():
                        down(source, k, zs).start()

    for j in range(1, group):
        @pl.loop(0, layers)
        def _(layer):
            @pl.loop(0, a_count)
            def _(k):
                arrived(layer * group + lax.rem(g + j, group), k)

    def left(source, k, layer):
        @pl.when((layer <= z) & (z + 1 < layers))
        def _():
            up(source, k, zs).wait_send()

        @pl.when((layer > z) & (z > 0))
        def _():
            down(source, k, zs).wait_send()

        @pl.when((layer == z) & (z > 0))
        def _():
            down(source, k, os).wait_send()

    @pl.loop(0, a_count)
    def _(k):

        @pl.loop(0, layers)
        def _(layer):
            source = layer * group + g
            left(source, k, layer)
            for j in range(1, group):
                across(source, k, j).wait_send()

    @pl.loop(0, k_count - a_count)
    def _(q):
        k = (q,)
        for j in range(1, group):
            across(s, k, j).wait_send()

        @pl.loop(0, layers)
        def _(layer):
            for j in range(group):
                left(layer * group + lax.rem(g + j, group), k, layer)

    for j in range(1, n):
        norm_copy(j).wait_recv()
    total_lines = norm.shape[0]
    for r in range(total_lines):
        if lines * n == total_lines:
            row = shares[r // lines, r % lines]
        else:
            many = n // total_lines
            row = shares[r * many, 0]
            for i in range(1, many):
                row = row + shares[r * many + i, 0]
        share[lines + r] = row
    norm[...] = share[pl.ds(lines, total_lines), 0, :].astype(norm.dtype)
    for j in range(1, width):
        piece_copy(j).wait_send()
    for j in range(1, n):
        max_copy(0, j).wait_send()
        max_copy(1, j).wait_send()
        norm_copy(j).wait_send()


def finish_kernel(n, out, whole, scale, norm, gate, up, whole_gate, whole_up, scale_gate, scale_up, serve, sem):
    held = whole.shape[0] // 2
    copies = []
    for i in range(n):
        for m, target in enumerate((gate, up)):
            copies.append((out.at[i, pl.ds(m * held, held)], target.at[pl.ds(i * held, held)]))
    for m, target in enumerate((whole_gate, whole_up)):
        copies.append((whole.at[pl.ds(m * held, held)], target))
    for m, target in enumerate((scale_gate, scale_up)):
        copies.append((scale.at[m], target))
    copies.append((norm, serve))
    copies = [pltpu.make_async_copy(a, b, sem.at[i]) for i, (a, b) in enumerate(copies)]
    for c in copies:
        c.start()
    for c in copies:
        c.wait()


def solution(mesh):
    n, width = mesh.shape["shard"], mesh.shape["width"]
    layers = math.gcd(n, math.isqrt(2 * n))
    group = n // layers

    def body(
        weight_gate, moment_gate, square_gate, weight_up, moment_up, square_up, norm_train, norm_step
    ):
        count = norm_train.shape[0]
        arrays = (
            weight_gate, moment_gate, square_gate, weight_up, moment_up, square_up,
            norm_train[None, :], norm_step[None, :],
        )
        held, columns = weight_gate.shape
        units = 2 * held // UNIT
        late_units = max(1, units * 5 // 32)
        early_units = units - late_units
        step = max(d for d in range(1, MOST + 1) if early_units % d == 0)
        rows, late_rows = step * UNIT, late_units * UNIT
        a_count, k_count = early_units // step, early_units // step + 1
        lines = max(1, width * count // 128)
        total_lines = n * width * count // 128
        loads = held // LOAD
        any_space = pl.BlockSpec(memory_space=pl.ANY)
        hbm_space = pl.BlockSpec(memory_space=pltpu.HBM)
        vmem_space = pl.BlockSpec(memory_space=pltpu.VMEM)
        dma = pltpu.SemaphoreType.DMA
        f32, bf16 = jnp.float32, jnp.bfloat16
        results = pl.pallas_call(
            functools.partial(
                gather_kernel, n, width, layers, group, rows, late_rows, a_count, k_count, count
            ),
            out_shape=(
                jax.ShapeDtypeStruct((n, 2 * held, columns), bf16),
                jax.ShapeDtypeStruct((2 * held, columns), f32),
                jax.ShapeDtypeStruct((2, 1, columns), f32),
                jax.ShapeDtypeStruct((total_lines, 128), bf16),
            ),
            in_specs=[hbm_space] * 8,
            out_specs=(vmem_space,) * 4,
            scratch_shapes=[
                pltpu.VMEM((2 * held, columns), f32),
                pltpu.VMEM((2 * held, columns), f32),
                pltpu.VMEM((2, 1, columns), f32),
                pltpu.VMEM((2, n, 1, columns), f32),
                pltpu.VMEM((2, 1, columns), f32),
                pltpu.VMEM((2, 1, count), f32),
                pltpu.VMEM((width, 1, 128), f32),
                pltpu.VMEM((lines + total_lines, 1, 128), f32),
                pltpu.VMEM((n, lines, 1, 128), f32),
                dma((2, 3, loads)),
                dma((2,)),
                dma((2, n)),
                dma((2, n)),
                dma((width,)),
                dma((width,)),
                dma((n,)),
                dma((n,)),
                dma((n, k_count)),
                dma((n, k_count)),
                dma((max(1, group - 1), n, k_count)),
                dma((n, k_count)),
            ],
            compiler_params=pltpu.CompilerParams(
                collective_id=0, has_side_effects=True, vmem_limit_bytes=VMEM_LIMIT
            ),
            name="gather",
        )(*(pltpu.with_memory_space_constraint(a, pltpu.HBM) for a in arrays))
        gate, up, whole_gate, whole_up, scale_gate, scale_up, serve = pl.pallas_call(
            functools.partial(finish_kernel, n),
            out_shape=(
                jax.ShapeDtypeStruct((n * held, columns), bf16),
                jax.ShapeDtypeStruct((n * held, columns), bf16),
                jax.ShapeDtypeStruct((held, columns), f32),
                jax.ShapeDtypeStruct((held, columns), f32),
                jax.ShapeDtypeStruct((1, columns), f32),
                jax.ShapeDtypeStruct((1, columns), f32),
                jax.ShapeDtypeStruct((total_lines, 128), bf16),
            ),
            in_specs=[any_space] * 4,
            out_specs=(hbm_space,) * 7,
            scratch_shapes=[dma((2 * n + 5,))],
            compiler_params=pltpu.CompilerParams(vmem_limit_bytes=1 << 20),
            name="finish",
        )(*results)
        return (
            gate, up, scale_gate.reshape(columns), scale_up.reshape(columns), serve.reshape(-1), whole_gate, whole_up
        )

    return jax.shard_map(
        body,
        mesh=mesh,
        in_specs=(P("shard", "width"),) * 6 + (P(("shard", "width")),) * 2,
        out_specs=(
            P(None, "width"),
            P(None, "width"),
            P("width"),
            P("width"),
            P(),
            P("shard", "width"),
            P("shard", "width"),
        ),
        check_vma=False,
    )
```

time: 189 us -> 182 us (0.963)
  Pallas kernels: 173 us -> 181 us
  local copies, waits for them, and re-layouts: 7.75 us -> 0 us
  other arithmetic: 7.37 us -> 0 us
    pallas_call x0 -> x1, Pallas kernels: none -> 7.31 us  [body(): pl.pallas_call(functools.partial(finish_kernel, n), out_shape=(jax.ShapeD...]
    slice x3 -> x0, local copies, waits for them, and re-layouts: 7.05 us -> none  [the longest x1 6.39 us: body(): out[:, held:].reshape(n * held, columns)]
    reduce_max x1 -> x0, other arithmetic: 6.67 us -> none  [body(): jnp.max(jnp.abs(whole_up), axis=0)]
where the time goes in v1:
time: 182 us
  Pallas kernels  181 us (99%)
    pallas_call x1, Pallas kernels, body(): pl.pallas_call(functools.partial(gather_kernel, n, width, layers, group,...  174 us
    pallas_call x1, Pallas kernels, body(): pl.pallas_call(functools.partial(finish_kernel, n), out_shape=(jax.ShapeD...  7.31 us

profile of v1, /device:TPU:0, one launch (start us, length us, event | category | flops | bytes accessed | tf_op | source)
XLA Modules:
  0.0 182.1 jit_solution(11887756376901251534)
XLA Ops:
  0.6 174.1 %gather.1 = (bf16[8,512,2048]{2,1,0:T(8,128)(2,1)S(1)}, f32[512,2048]{1,0:T(8,128)S(1)}, f32[2,1,2048]{2,1,0:T(1,128)S(1)}, bf16[16,128]{1,0:T(8,128)(2,1)S(1)}) custom-call(f32[256,2048]{1,0:T(8,128)} %wg.1, f32[256,2048]{1,0:T(8,128)} %mg.1, f32[256,2048]{1,0:T(8,128)} %sg.1, f32[256,2048]{1,0:T(8,128)} %wu.1, f32[256,2048]{1,0:T(8,128)} %mu.1, ...), custom_call_target="tpu_custom_call" | custom-call | tf_op jit(solution)/shard_map/gather/pallas_call | solution.py:383
  174.8 7.3 %finish.1 = (bf16[2048,2048]{1,0:T(8,128)(2,1)}, bf16[2048,2048]{1,0:T(8,128)(2,1)}, f32[256,2048]{1,0:T(8,128)}, f32[256,2048]{1,0:T(8,128)}, f32[1,2048]{1,0:T...) custom-call(bf16[8,512,2048]{2,1,0:T(8,128)(2,1)S(1)} %get-tuple-element.18.out, ...), custom_call_target="tpu_custom_call" | custom-call | tf_op jit(solution)/shard_map/finish/pallas_call | solution.py:423

commit v2 on v1

v2 whole, which is shorter than its diff:
```python
import functools
import math

import jax
import jax.numpy as jnp
from jax import lax
from jax.experimental import pallas as pl
from jax.experimental.pallas import tpu as pltpu
from jax.sharding import PartitionSpec as P

MESH = pl.DeviceIdType.MESH
learn_rate = 0.02
decay_rate = 0.1
tiny_value = 1e-08
UNIT = 16
TILE = 8
RAW = 24
PARTS = 4
LOAD = 32
BLOCK = 8
VMEM_LIMIT = 12 << 20


def gather_kernel(
    n, width, layers, group, chunks, count,
    wg, mg, sg, wu, mu, su, train, change,
    out, whole, scale_ref, norm,
    moment, square, mx, maxbuf, inv, terms, pieces, share, shares, land,
    in_sem, term_sem, ms, mr, ns1, nr1, ns2, nr2, us, ds, ys, yr, zr, zl, es, er,
):
    s, w = lax.axis_index("shard"), lax.axis_index("width")
    z, g = s // group, lax.rem(s, group)
    above, below = lax.rem(s + group, n), lax.rem(s + n - group, n)
    raw = chunks[0][1]
    held, columns = wg.shape
    loads = held // LOAD
    parts = ((wg, whole), (mg, moment), (sg, square)), ((wu, whole), (mu, moment), (su, square))

    def load(m, i, c):
        source, target = parts[m][i]
        at = pl.multiple_of(c * LOAD, LOAD)
        return pltpu.make_async_copy(
            source.at[pl.ds(at, LOAD)], target.at[pl.ds(m * held + at, LOAD)], in_sem.at[m, c]
        )

    for i, ref in enumerate((train, change)):
        pltpu.make_async_copy(ref, terms.at[i], term_sem.at[0]).start()
    for m in range(2):
        @pl.loop(0, loads)
        def _(c):
            for i in range(3):
                load(m, i, c).start()

    barrier = pltpu.get_barrier_semaphore()
    for j in range(1, n):
        pl.semaphore_signal(barrier, inc=1, device_id=(lax.rem(s + j, n), w), device_id_type=MESH)
    for j in range(1, width):
        pl.semaphore_signal(barrier, inc=1, device_id=(s, lax.rem(w + j, width)), device_id_type=MESH)

    def max_copy(m, j):
        return pltpu.make_async_remote_copy(
            mx.at[m], maxbuf.at[m, s], ms.at[m], mr.at[m],
            device_id=(lax.rem(s + j, n), w), device_id_type=MESH,
        )

    def partner(j):
        return z * group + lax.rem(g + j, group)

    def raw_copy(lane):
        device = (above, below)[lane] if lane < 2 else partner(lane - 1)
        return pltpu.make_async_remote_copy(
            whole.at[pl.ds(0, raw)], land.at[lane], es.at[lane], er.at[lane],
            device_id=(device, w), device_id_type=MESH,
        )

    def piece_copy(j):
        return pltpu.make_async_remote_copy(
            pieces.at[w], pieces.at[w], ns1.at[0], nr1.at[0],
            device_id=(s, lax.rem(w + j, width)), device_id_type=MESH,
        )

    def norm_copy(j):
        return pltpu.make_async_remote_copy(
            shares.at[s], shares.at[s], ns2.at[0], nr2.at[0],
            device_id=(lax.rem(s + j, n), w), device_id_type=MESH,
        )

    trio = moment.at[pl.ds(0, 3 * LOAD)]

    def update(m):
        def chunk(c, top):
            pltpu.make_async_copy(trio, trio, in_sem.at[m, c]).wait()

            def block(b, top):
                at = pl.ds(pl.multiple_of(m * held + c * LOAD + b * BLOCK, BLOCK), BLOCK)
                old = whole[at, :]
                new = old - learn_rate * (moment[at, :] / (jnp.sqrt(square[at, :]) + tiny_value) + decay_rate * old)
                whole[at, :] = new
                return jnp.maximum(top, jnp.abs(new))

            return lax.fori_loop(0, LOAD // BLOCK, block, top)

        top = lax.fori_loop(0, loads, chunk, jnp.zeros((BLOCK, columns), jnp.float32))
        mx[m] = jnp.max(top, axis=0, keepdims=True)

    def scale(m):
        others = maxbuf.at[m, pl.ds(0, n - 1)]
        pltpu.make_async_copy(others, others, mr.at[m]).wait()
        top = mx[m]
        for j in range(1, n):
            top = jnp.maximum(top, maxbuf[m, lax.rem(s + n - j, n)])
        scale_ref[m] = top
        inv[m] = 1.0 / top

    update(0)
    lane = lax.broadcasted_iota(jnp.int32, (1, 128), 1)
    per = 128 // count
    spot = lax.rem(s * width + w, per)
    pltpu.make_async_copy(terms, terms, term_sem.at[0]).wait()
    piece = jnp.concatenate([terms[0] + terms[1]] * per, axis=1)
    pieces[w] = jnp.where(lane // count == spot, piece, 0.0)
    pl.semaphore_wait(barrier, n - 1 + width - 1)
    for j in range(1, n):
        max_copy(0, j).start()

    @pl.when(z + 1 < layers)
    def _():
        raw_copy(0).start()

    @pl.when(z > 0)
    def _():
        raw_copy(1).start()

    for j in range(1, group):
        raw_copy(1 + j).start()
    for j in range(1, width):
        piece_copy(j).start()
    update(1)
    for j in range(1, n):
        max_copy(1, j).start()
    last = len(chunks) - 1

    def place(source, k):
        start, size = chunks[k]
        return out.at[source, pl.ds(start, size)]

    def kind(k):
        return 0 if k == 0 else 2 if k == last else 1

    def copy(source, k, send, recv, device):
        return pltpu.make_async_remote_copy(
            place(source, k), place(source, k), send, recv, device_id=(device, w), device_id_type=MESH
        )

    def landed(source, k):
        return zl.at[source] if k == last else zr.at[source // group, k]

    def up(source, k):
        return copy(source, k, us.at[kind(k)], landed(source, k), above)

    def down(source, k):
        return copy(source, k, ds.at[kind(k)], landed(source, k), below)

    def across(source, k, j):
        recv = zl.at[source] if k == last else yr.at[j - 1, kind(k)]
        return copy(source, k, ys.at[j - 1, kind(k)], recv, partner(j))

    def across_all(source, k):
        for j in range(1, group):
            across(source, k, j).start()

    def arrived(source, k):
        pltpu.make_async_copy(place(source, k), place(source, k), landed(source, k)).wait()

    def settle(sem, many, size):
        block = out.at[pl.ds(0, many), pl.ds(0, size)]
        pltpu.make_async_copy(block, block, sem).wait()

    def divide(m, unit):
        at = pl.ds(pl.multiple_of(unit * UNIT, UNIT), UNIT)
        out[s, at, :] = (whole[at, :] * inv[m]).astype(out.dtype)

    per_matrix = held // UNIT
    done = 0
    scale(0)

    def divide_to(limit):
        nonlocal done
        for m in range(2):
            first, stop = max(done, m * per_matrix), min(limit, (m + 1) * per_matrix)
            if first < stop:
                if m == 1 and done <= per_matrix:
                    scale(1)

                @pl.loop(first, stop)
                def _(u):
                    divide(m, u)

                done = stop

    for k in range(1, last):
        divide_to(-(-sum(chunks[k]) // UNIT))

        @pl.when(z + 1 < layers)
        def _():
            up(s, k).start()

        @pl.when(z > 0)
        def _():
            down(s, k).start()

        across_all(s, k)

    divide_to(2 * held // UNIT)
    across_all(s, last)

    others = pieces.at[pl.ds(0, width - 1)]
    pltpu.make_async_copy(others, others, nr1.at[0]).wait()
    lines = max(1, width // per)
    for r in range(lines):
        total = pieces[r * (width // lines)]
        for i in range(1, width // lines):
            total = total + pieces[r * (width // lines) + i]
        share[r] = total
        shares[s, r] = total
    for j in range(1, n):
        norm_copy(j).start()

    def take(lane, source):
        raw_copy(lane).wait_recv()
        out[source, pl.ds(0, raw), :] = (land[lane] * inv[0]).astype(out.dtype)

    for d in range(1, layers):
        for k in range(last):
            @pl.when(z - d >= 0)
            def _():
                source = s - d * group
                take(0, source) if d == 1 and k == 0 else arrived(source, k)

                @pl.when(z + 1 < layers)
                def _():
                    up(source, k).start()

                across_all(source, k)

            @pl.when(z + d < layers)
            def _():
                source = s + d * group
                take(1, source) if d == 1 and k == 0 else arrived(source, k)

                @pl.when(z > 0)
                def _():
                    down(source, k).start()

                across_all(source, k)

            if d == 1 and k == 0:
                for j in range(1, group):
                    take(1 + j, partner(group - j))

    if layers == 1:
        for j in range(1, group):
            take(1 + j, partner(group - j))

    for j in range(group):
        source = partner(j)
        if j:
            arrived(source, last)

        @pl.when(z + 1 < layers)
        def _():
            up(source, last).start()

        @pl.when(z > 0)
        def _():
            down(source, last).start()

    for d in range(1, layers):
        for j in range(group):
            @pl.when(z - d >= 0)
            def _():
                source = partner(j) - d * group
                arrived(source, last)

                @pl.when(z + 1 < layers)
                def _():
                    up(source, last).start()

            @pl.when(z + d < layers)
            def _():
                source = partner(j) + d * group
                arrived(source, last)

                @pl.when(z > 0)
                def _():
                    down(source, last).start()

    early = sum(chunks[last - 1])
    tail = chunks[last][1]
    for sems in (yr, ys):
        for j in range(1, group):
            if layers > 1:
                settle(sems.at[j - 1, 0], layers - 1, raw)
            settle(sems.at[j - 1, 1], layers, early - raw)
    for j in range(1, group):
        settle(ys.at[j - 1, 2], 1, tail)
    for level in range(layers):
        @pl.when(z == level)
        def _():
            for sems, more, many in ((us, layers - 1 - level, level), (ds, level, layers - 1 - level)):
                if more:
                    if many:
                        settle(sems.at[0], many, raw)
                    settle(sems.at[1], many + 1, early - raw)
                    settle(sems.at[2], (many + 1) * group, tail)

    @pl.when(z + 1 < layers)
    def _():
        raw_copy(0).wait_send()

    @pl.when(z > 0)
    def _():
        raw_copy(1).wait_send()

    for j in range(1, group):
        raw_copy(1 + j).wait_send()

    others = shares.at[pl.ds(0, n - 1)]
    pltpu.make_async_copy(others, others, nr2.at[0]).wait()
    total_lines = norm.shape[0]
    for r in range(total_lines):
        if lines * n == total_lines:
            row = shares[r // lines, r % lines]
        else:
            many = n // total_lines
            row = shares[r * many, 0]
            for i in range(1, many):
                row = row + shares[r * many + i, 0]
        share[lines + r] = row
    norm[...] = share[pl.ds(lines, total_lines), 0, :].astype(norm.dtype)
    pltpu.make_async_copy(others, others, ns2.at[0]).wait()
    for m in range(2):
        block = maxbuf.at[m, pl.ds(0, n - 1)]
        pltpu.make_async_copy(block, block, ms.at[m]).wait()
    block = pieces.at[pl.ds(0, width - 1)]
    pltpu.make_async_copy(block, block, ns1.at[0]).wait()


def finish_kernel(out, whole, scale, norm, gate, up, whole_gate, whole_up, scale_gate, scale_up, serve, sem):
    held = whole.shape[0] // 2
    copies = []
    for m, target in enumerate((gate, up)):
        copies.append((out.at[:, pl.ds(m * held, held)], target))
    for m, target in enumerate((whole_gate, whole_up)):
        copies.append((whole.at[pl.ds(m * held, held)], target))
    for m, target in enumerate((scale_gate, scale_up)):
        copies.append((scale.at[m], target))
    copies.append((norm, serve))
    copies = [pltpu.make_async_copy(a, b, sem.at[i]) for i, (a, b) in enumerate(copies)]
    for c in copies:
        c.start()
    for c in copies:
        c.wait()


def solution(mesh):
    n, width = mesh.shape["shard"], mesh.shape["width"]
    layers = math.gcd(n, math.isqrt(2 * n))
    group = n // layers

    def body(
        weight_gate, moment_gate, square_gate, weight_up, moment_up, square_up, norm_train, norm_step
    ):
        count = norm_train.shape[0]
        arrays = (
            weight_gate, moment_gate, square_gate, weight_up, moment_up, square_up,
            norm_train[None, :], norm_step[None, :],
        )
        held, columns = weight_gate.shape
        late = -(-held // (3 * TILE)) * TILE
        early = 2 * held - late
        cuts = [0, RAW] + [early * i // (PARTS * TILE) * TILE for i in range(1, PARTS)] + [early, 2 * held]
        chunks = tuple((start, stop - start) for start, stop in zip(cuts, cuts[1:]))
        k_count = len(chunks)
        lines = max(1, width * count // 128)
        total_lines = n * width * count // 128
        loads = held // LOAD
        any_space = pl.BlockSpec(memory_space=pl.ANY)
        hbm_space = pl.BlockSpec(memory_space=pltpu.HBM)
        vmem_space = pl.BlockSpec(memory_space=pltpu.VMEM)
        dma = pltpu.SemaphoreType.DMA
        f32, bf16 = jnp.float32, jnp.bfloat16
        results = pl.pallas_call(
            functools.partial(
                gather_kernel, n, width, layers, group, chunks, count
            ),
            out_shape=(
                jax.ShapeDtypeStruct((n, 2 * held, columns), bf16),
                jax.ShapeDtypeStruct((2 * held, columns), f32),
                jax.ShapeDtypeStruct((2, 1, columns), f32),
                jax.ShapeDtypeStruct((total_lines, 128), bf16),
            ),
            in_specs=[hbm_space] * 8,
            out_specs=(vmem_space,) * 4,
            scratch_shapes=[
                pltpu.VMEM((2 * held, columns), f32),
                pltpu.VMEM((2 * held, columns), f32),
                pltpu.VMEM((2, 1, columns), f32),
                pltpu.VMEM((2, n, 1, columns), f32),
                pltpu.VMEM((2, 1, columns), f32),
                pltpu.VMEM((2, 1, count), f32),
                pltpu.VMEM((width, 1, 128), f32),
                pltpu.VMEM((lines + total_lines, 1, 128), f32),
                pltpu.VMEM((n, lines, 1, 128), f32),
                pltpu.VMEM((group + 1, RAW, columns), f32),
                dma((2, loads)),
                dma((1,)),
                dma((2,)),
                dma((2,)),
                dma((1,)),
                dma((1,)),
                dma((1,)),
                dma((1,)),
                dma((3,)),
                dma((3,)),
                dma((max(1, group - 1), 3)),
                dma((max(1, group - 1), 2)),
                dma((layers, k_count - 1)),
                dma((n,)),
                dma((group + 1,)),
                dma((group + 1,)),
            ],
            compiler_params=pltpu.CompilerParams(
                collective_id=0, has_side_effects=True, vmem_limit_bytes=VMEM_LIMIT
            ),
            name="gather",
        )(*(pltpu.with_memory_space_constraint(a, pltpu.HBM) for a in arrays))
        gate, up, whole_gate, whole_up, scale_gate, scale_up, serve = pl.pallas_call(
            finish_kernel,
            out_shape=(
                jax.ShapeDtypeStruct((n, held, columns), bf16),
                jax.ShapeDtypeStruct((n, held, columns), bf16),
                jax.ShapeDtypeStruct((held, columns), f32),
                jax.ShapeDtypeStruct((held, columns), f32),
                jax.ShapeDtypeStruct((1, columns), f32),
                jax.ShapeDtypeStruct((1, columns), f32),
                jax.ShapeDtypeStruct((total_lines, 128), bf16),
            ),
            in_specs=[any_space] * 4,
            out_specs=(hbm_space,) * 7,
            scratch_shapes=[dma((7,))],
            compiler_params=pltpu.CompilerParams(vmem_limit_bytes=1 << 20),
            name="finish",
        )(*results)
        return (
            gate.reshape(-1, columns), up.reshape(-1, columns), scale_gate.reshape(-1), scale_up.reshape(-1),
            serve.reshape(-1), whole_gate, whole_up,
        )

    return jax.shard_map(
        body,
        mesh=mesh,
        in_specs=(P("shard", "width"),) * 6 + (P(("shard", "width")),) * 2,
        out_specs=(
            P(None, "width"),
            P(None, "width"),
            P("width"),
            P("width"),
            P(),
            P("shard", "width"),
            P("shard", "width"),
        ),
        check_vma=False,
    )
```

time: 182 us -> 178 us (0.978)
  Pallas kernels: 181 us -> 178 us
    pallas_call x1, Pallas kernels: 174 us -> 170 us  [body(): pl.pallas_call(functools.partial(gather_kernel, n, width, layers, group,...]
where the time goes in v2:
time: 178 us
  Pallas kernels  178 us (100%)
    pallas_call x1, Pallas kernels, body(): pl.pallas_call(functools.partial(gather_kernel, n, width, layers, group,...  170 us
    pallas_call x1, Pallas kernels, body(): pl.pallas_call(finish_kernel, out_shape=(jax.ShapeDtypeStruct((n, held, c...  7.3 us

profile of v2, /device:TPU:0, one launch (start us, length us, event | category | flops | bytes accessed | tf_op | source)
XLA Modules:
  0.0 178.2 jit_solution(9685448666383660243)
XLA Ops:
  0.6 170.2 %gather.1 = (bf16[8,512,2048]{2,1,0:T(8,128)(2,1)S(1)}, f32[512,2048]{1,0:T(8,128)S(1)}, f32[2,1,2048]{2,1,0:T(1,128)S(1)}, bf16[16,128]{1,0:T(8,128)(2,1)S(1)}) custom-call(f32[256,2048]{1,0:T(8,128)} %wg.1, f32[256,2048]{1,0:T(8,128)} %mg.1, f32[256,2048]{1,0:T(8,128)} %sg.1, f32[256,2048]{1,0:T(8,128)} %wu.1, f32[256,2048]{1,0:T(8,128)} %mu.1, ...), custom_call_target="tpu_custom_call" | custom-call | tf_op jit(solution)/shard_map/gather/pallas_call | solution.py:393
  170.9 7.3 %finish.1 = (bf16[8,256,2048]{2,1,0:T(8,128)(2,1)}, bf16[8,256,2048]{2,1,0:T(8,128)(2,1)}, f32[256,2048]{1,0:T(8,128)}, f32[256,2048]{1,0:T(8,128)}, f32[1,2048]...) custom-call(bf16[8,512,2048]{2,1,0:T(8,128)(2,1)S(1)} %get-tuple-element.18.out, ...), custom_call_target="tpu_custom_call" | custom-call | tf_op jit(solution)/shard_map/finish/pallas_call | solution.py:438

commit v3 on v2

v3 whole, which is shorter than its diff:
```python
import functools
import math

import jax
import jax.numpy as jnp
from jax import lax
from jax.experimental import pallas as pl
from jax.experimental.pallas import tpu as pltpu
from jax.sharding import PartitionSpec as P

MESH = pl.DeviceIdType.MESH
learn_rate = 0.02
decay_rate = 0.1
tiny_value = 1e-08
UNIT = 16
TILE = 8
RAW = 32
ENDS = 40
SIDES = 64
PARTS = 2
SPLIT = 2
LOAD = 32
BLOCK = 8
VMEM_LIMIT = 12 << 20
FLOPS = 100_000_000


def gather_kernel(
    n, width, layers, group, chunks, hidden, count,
    wg, mg, sg, wu, mu, su, train, change,
    out, whole, scale_ref, norm, ends, sides,
    moment, square, mx, maxbuf, inv, terms, pieces, share, shares, land,
    in_sem, term_sem, ms, mr, ns1, nr1, ns2, nr2, us, ds, ys, yr, zr, zl, es, er,
):
    s, w = lax.axis_index("shard"), lax.axis_index("width")
    z, g = s // group, lax.rem(s, group)
    above, below = lax.rem(s + group, n), lax.rem(s + n - group, n)
    raw = chunks[0][1]
    held, columns = wg.shape
    half = columns // SPLIT
    trios = ((wg, whole), (mg, moment), (sg, square)), ((wu, whole), (mu, moment), (su, square))
    phases = [(0, i * half, half) for i in range(SPLIT)] + [(1, 0, columns)]

    def load(p, i, c):
        m, left, size = phases[p]
        source, target = trios[m][i]
        rows = LOAD * columns // size
        at = pl.multiple_of(c * rows, rows)
        cols = pl.ds(left, size)
        return pltpu.make_async_copy(
            source.at[pl.ds(at, rows), cols], target.at[pl.ds(m * held + at, rows), cols], in_sem.at[p, c]
        )

    def loads(p):
        return held * phases[p][2] // (LOAD * columns)

    for i, ref in enumerate((train, change)):
        pltpu.make_async_copy(ref, terms.at[i], term_sem.at[0]).start()
    for p in range(len(phases)):
        @pl.loop(0, loads(p))
        def _(c):
            for i in range(3):
                load(p, i, c).start()

    barrier = pltpu.get_barrier_semaphore()
    for j in range(1, n):
        pl.semaphore_signal(barrier, inc=1, device_id=(lax.rem(s + j, n), w), device_id_type=MESH)
    for j in range(1, width):
        pl.semaphore_signal(barrier, inc=1, device_id=(s, lax.rem(w + j, width)), device_id_type=MESH)

    def max_copy(p, j):
        m, left, size = phases[p]
        cols = pl.ds(left, size)
        return pltpu.make_async_remote_copy(
            mx.at[m, :, cols], maxbuf.at[m, s, :, cols], ms.at[0], mr.at[p],
            device_id=(lax.rem(s + j, n), w), device_id_type=MESH,
        )

    def max_send(p):
        for j in range(1, n):
            max_copy(p, j).start()

    def partner(j):
        return z * group + lax.rem(g + j, group)

    def raw_copy(lane):
        device = (above, below)[lane] if lane < 2 else partner(lane - 1)
        return pltpu.make_async_remote_copy(
            whole.at[pl.ds(0, raw), pl.ds(0, half)], land.at[lane], es.at[lane], er.at[lane],
            device_id=(device, w), device_id_type=MESH,
        )

    def piece_copy(j):
        return pltpu.make_async_remote_copy(
            pieces.at[w], pieces.at[w], ns1.at[0], nr1.at[0],
            device_id=(s, lax.rem(w + j, width)), device_id_type=MESH,
        )

    def norm_copy(j):
        return pltpu.make_async_remote_copy(
            shares.at[s], shares.at[s], ns2.at[0], nr2.at[0],
            device_id=(lax.rem(s + j, n), w), device_id_type=MESH,
        )

    trio = moment.at[pl.ds(0, 3 * LOAD)]

    def update(p):
        m, left, size = phases[p]
        cols = pl.ds(left, size)
        rows = LOAD * columns // size

        def chunk(c, top):
            pltpu.make_async_copy(trio, trio, in_sem.at[p, c]).wait()

            def block(b, top):
                at = pl.ds(pl.multiple_of(m * held + c * rows + b * BLOCK, BLOCK), BLOCK)
                old = whole[at, cols]
                new = old - learn_rate * (moment[at, cols] / (jnp.sqrt(square[at, cols]) + tiny_value) + decay_rate * old)
                whole[at, cols] = new
                return jnp.maximum(top, jnp.abs(new))

            return lax.fori_loop(0, rows // BLOCK, block, top)

        top = lax.fori_loop(0, loads(p), chunk, jnp.zeros((BLOCK, size), jnp.float32))
        mx[m, :, cols] = jnp.max(top, axis=0, keepdims=True)

    def scale(p):
        m, left, size = phases[p]
        cols = pl.ds(left, size)
        others = maxbuf.at[m, pl.ds(0, n - 1), :, cols]
        pltpu.make_async_copy(others, others, mr.at[p]).wait()
        top = mx[m, :, cols]
        for j in range(1, n):
            top = jnp.maximum(top, maxbuf[m, lax.rem(s + n - j, n), :, cols])
        scale_ref[m, :, cols] = top
        inv[m, :, cols] = 1.0 / top

    update(0)
    pl.semaphore_wait(barrier, n - 1 + width - 1)
    max_send(0)

    def raw_all(act):
        if raw:
            @pl.when(z + 1 < layers)
            def _():
                act(raw_copy(0))

            @pl.when(z > 0)
            def _():
                act(raw_copy(1))

            for j in range(1, group):
                act(raw_copy(1 + j))

    raw_all(lambda c: c.start())
    for p in range(1, SPLIT):
        update(p)
        max_send(p)
    lane = lax.broadcasted_iota(jnp.int32, (1, 128), 1)
    per = 128 // count
    spot = lax.rem(s * width + w, per)
    pltpu.make_async_copy(terms, terms, term_sem.at[0]).wait()
    piece = jnp.concatenate([terms[0] + terms[1]] * per, axis=1)
    pieces[w] = jnp.where(lane // count == spot, piece, 0.0)
    for j in range(1, width):
        piece_copy(j).start()

    late, tail = len(chunks) - 2, len(chunks) - 1
    side = late - 1 if hidden else -1
    lates = (late, tail) if hidden else (late,)

    def place(source, k):
        start, size, left, wide = chunks[k]
        return out.at[source, pl.ds(start, size), pl.ds(left, wide)]

    def kind(k):
        return 0 if k == 0 else 1 if k < late else k - late + 2

    def copy(source, k, send, recv, device):
        return pltpu.make_async_remote_copy(
            place(source, k), place(source, k), send, recv, device_id=(device, w), device_id_type=MESH
        )

    def landed(source, k):
        return zl.at[source, k - late] if k >= late else zr.at[source // group, k]

    def up(source, k):
        return copy(source, k, us.at[kind(k)], landed(source, k), above)

    def down(source, k):
        return copy(source, k, ds.at[kind(k)], landed(source, k), below)

    def across(source, k, j):
        spot = 4 if k == side else kind(k)
        recv = zl.at[source, k - late] if k >= late else yr.at[j - 1, spot]
        return copy(source, k, ys.at[j - 1, spot], recv, partner(j))

    def across_all(source, k):
        for j in range(1, group):
            across(source, k, j).start()

    def arrived(source, k):
        pltpu.make_async_copy(place(source, k), place(source, k), landed(source, k)).wait()

    def settle(sem, many, size):
        block = out.at[pl.ds(0, many), pl.ds(0, size)]
        pltpu.make_async_copy(block, block, sem).wait()

    def divide(start, stop, left, wide):
        m = start // held
        cols = pl.ds(left, wide)

        @pl.loop(start // UNIT, stop // UNIT)
        def _(u):
            at = pl.ds(pl.multiple_of(u * UNIT, UNIT), UNIT)
            out[s, at, cols] = (whole[at, cols] * inv[m, :, cols]).astype(out.dtype)

    def send(k):
        @pl.when(z + 1 < layers)
        def _():
            up(s, k).start()

        @pl.when(z > 0)
        def _():
            down(s, k).start()

        if k != side:
            across_all(s, k)

    done = held
    for k in range(1, late):
        start, size, left, wide = chunks[k]
        if start < held:
            scale(left // half)
            divide(0, held, left, wide)
            send(k)
            if k == 1:
                update(SPLIT)
                max_send(SPLIT)
        else:
            if done == held:
                scale(SPLIT)
            stop = -(-(start + size) // UNIT) * UNIT
            divide(done, stop, 0, columns)
            done = stop
            send(k)
    if done == held:
        scale(SPLIT)
    divide(done, 2 * held, 0, columns)
    for k in lates:
        across_all(s, k)
    if hidden:
        sides[...] = place(s, side)[...]
        ends[pl.ds(0, chunks[tail][1]), :] = place(s, tail)[...]

    others = pieces.at[pl.ds(0, width - 1)]
    pltpu.make_async_copy(others, others, nr1.at[0]).wait()
    lines = max(1, width // per)
    for r in range(lines):
        total = pieces[r * (width // lines)]
        for i in range(1, width // lines):
            total = total + pieces[r * (width // lines) + i]
        share[r] = total
        shares[s, r] = total
    for j in range(1, n):
        norm_copy(j).start()

    def take(lane, source):
        raw_copy(lane).wait_recv()
        cols = pl.ds(0, half)
        out[source, pl.ds(0, raw), cols] = (land[lane] * inv[0, :, cols]).astype(out.dtype)

    for d in range(1, layers):
        for k in range(0 if raw else 1, late):
            @pl.when(z - d >= 0)
            def _():
                source = s - d * group
                take(0, source) if d == 1 and k == 0 else arrived(source, k)

                @pl.when(z + 1 < layers)
                def _():
                    up(source, k).start()

                across_all(source, k)

            @pl.when(z + d < layers)
            def _():
                source = s + d * group
                take(1, source) if d == 1 and k == 0 else arrived(source, k)

                @pl.when(z > 0)
                def _():
                    down(source, k).start()

                across_all(source, k)

            if d == 1 and k == 0:
                for j in range(1, group):
                    take(1 + j, partner(group - j))

    if layers == 1 and raw:
        for j in range(1, group):
            take(1 + j, partner(group - j))

    for j in range(group):
        source = partner(j)
        for k in lates:
            if j:
                arrived(source, k)
            cut = 1 if k == tail else 0

            @pl.when(z + 1 + cut < layers)
            def _():
                up(source, k).start()

            @pl.when(z > cut)
            def _():
                down(source, k).start()

        if hidden and j:
            size = chunks[tail][1]
            ends[pl.ds(j * size, size), :] = place(source, tail)[...]

    for d in range(1, layers):
        for j in range(group):
            for k in lates:
                cut = 1 if k == tail and d == 1 else 0

                @pl.when((z - d >= 0) & (z + cut < layers))
                def _():
                    source = partner(j) - d * group
                    arrived(source, k)

                    @pl.when(z + 1 < layers)
                    def _():
                        up(source, k).start()

                @pl.when((z + d < layers) & (z >= cut))
                def _():
                    source = partner(j) + d * group
                    arrived(source, k)

                    @pl.when(z > 0)
                    def _():
                        down(source, k).start()

    early = chunks[late][0]
    plain = chunks[side][0] if hidden else early
    raw_lines = raw // SPLIT
    for sems in (yr, ys):
        for j in range(1, group):
            if layers > 1 and raw:
                settle(sems.at[j - 1, 0], layers - 1, raw_lines)
            settle(sems.at[j - 1, 1], layers, plain - raw_lines)
            if hidden:
                settle(sems.at[j - 1, 4], layers - 1, early - plain)
    for j in range(1, group):
        for k in lates:
            settle(ys.at[j - 1, kind(k)], 1, chunks[k][1])
    for level in range(layers):
        @pl.when(z == level)
        def _():
            for sems, more, many in ((us, layers - 1 - level, level), (ds, level, layers - 1 - level)):
                if more:
                    if many and raw:
                        settle(sems.at[0], many, raw_lines)
                    settle(sems.at[1], many + 1, early - raw_lines)
                    for k in lates:
                        own = 0 if k == tail and more == 1 else 1
                        if many + own:
                            settle(sems.at[kind(k)], (many + own) * group, chunks[k][1])

    raw_all(lambda c: c.wait_send())

    others = shares.at[pl.ds(0, n - 1)]
    pltpu.make_async_copy(others, others, nr2.at[0]).wait()
    total_lines = norm.shape[0]
    for r in range(total_lines):
        if lines * n == total_lines:
            row = shares[r // lines, r % lines]
        else:
            many = n // total_lines
            row = shares[r * many, 0]
            for i in range(1, many):
                row = row + shares[r * many + i, 0]
        share[lines + r] = row
    norm[...] = share[pl.ds(lines, total_lines), 0, :].astype(norm.dtype)
    pltpu.make_async_copy(others, others, ns2.at[0]).wait()
    block = maxbuf.at[:, pl.ds(0, n - 1)]
    pltpu.make_async_copy(block, block, ms.at[0]).wait()
    block = pieces.at[pl.ds(0, width - 1)]
    pltpu.make_async_copy(block, block, ns1.at[0]).wait()


def finish_kernel(out, whole, scale, norm, gate, up, whole_gate, whole_up, scale_gate, scale_up, serve, sem):
    held = whole.shape[0] // 2
    copies = []
    for m, target in enumerate((gate, up)):
        copies.append((out.at[:, pl.ds(m * held, held)], target))
    for m, target in enumerate((whole_gate, whole_up)):
        copies.append((whole.at[pl.ds(m * held, held)], target))
    for m, target in enumerate((scale_gate, scale_up)):
        copies.append((scale.at[m], target))
    copies.append((norm, serve))
    copies = [pltpu.make_async_copy(a, b, sem.at[i]) for i, (a, b) in enumerate(copies)]
    for c in copies:
        c.start()
    for c in copies:
        c.wait()


def patch_kernel(layers, group, at, far, near, _, up, sem):
    s = lax.axis_index("shard")
    z, g = s // group, lax.rem(s, group)
    partner = z * group + lax.rem(g + 1, group)
    rows, sides = far.shape[0] // group, near.shape[0]
    held = up.shape[1]
    copies = [pltpu.make_async_copy(near, up.at[partner, pl.ds(at, sides)], sem.at[0])]
    base = jnp.where(z == 0, 1, layers - 2) * group
    ends = [
        pltpu.make_async_copy(
            far.at[pl.ds(j * rows, rows)],
            up.at[base + lax.rem(g + j, group), pl.ds(held - rows, rows)],
            sem.at[1 + j],
        )
        for j in range(group)
    ]
    copies[0].start()

    @pl.when((z == 0) | (z == layers - 1))
    def _():
        for c in ends:
            c.start()
        for c in ends:
            c.wait()

    copies[0].wait()


def solution(mesh):
    n, width = mesh.shape["shard"], mesh.shape["width"]
    layers = math.gcd(n, math.isqrt(2 * n))
    group = n // layers

    def body(
        weight_gate, moment_gate, square_gate, weight_up, moment_up, square_up, norm_train, norm_step
    ):
        count = norm_train.shape[0]
        arrays = (
            weight_gate, moment_gate, square_gate, weight_up, moment_up, square_up,
            norm_train[None, :], norm_step[None, :],
        )
        held, columns = weight_gate.shape
        hidden = layers > 2 and group == 2
        late = -(-held // (3 * TILE)) * TILE
        early = 2 * held - late
        ends = min(ENDS, late // (2 * TILE) * TILE)
        half = columns // SPLIT
        chunks = [(0, RAW, 0, half), (RAW, held - RAW, 0, half)]
        chunks += [(0, held, i * half, half) for i in range(1, SPLIT)]
        stop = early - SIDES if hidden else early
        cuts = [held + (stop - held) * i // (PARTS * TILE) * TILE for i in range(PARTS)] + [stop]
        cuts += [early, 2 * held - ends, 2 * held] if hidden else [2 * held]
        chunks += [(start, stop - start, 0, columns) for start, stop in zip(cuts, cuts[1:])]
        if not hidden:
            chunks.append(chunks[-1])
        chunks = tuple(chunks)
        k_count = len(chunks)
        lines = max(1, width * count // 128)
        total_lines = n * width * count // 128
        any_space = pl.BlockSpec(memory_space=pl.ANY)
        hbm_space = pl.BlockSpec(memory_space=pltpu.HBM)
        vmem_space = pl.BlockSpec(memory_space=pltpu.VMEM)
        dma = pltpu.SemaphoreType.DMA
        f32, bf16 = jnp.float32, jnp.bfloat16
        results = pl.pallas_call(
            functools.partial(
                gather_kernel, n, width, layers, group, chunks, hidden, count
            ),
            out_shape=(
                jax.ShapeDtypeStruct((n, 2 * held, columns), bf16),
                jax.ShapeDtypeStruct((2 * held, columns), f32),
                jax.ShapeDtypeStruct((2, 1, columns), f32),
                jax.ShapeDtypeStruct((total_lines, 128), bf16),
                jax.ShapeDtypeStruct((group * ends, columns), bf16),
                jax.ShapeDtypeStruct((SIDES, columns), bf16),
            ),
            in_specs=[hbm_space] * 8,
            out_specs=(vmem_space,) * 6,
            scratch_shapes=[
                pltpu.VMEM((2 * held, columns), f32),
                pltpu.VMEM((2 * held, columns), f32),
                pltpu.VMEM((2, 1, columns), f32),
                pltpu.VMEM((2, n, 1, columns), f32),
                pltpu.VMEM((2, 1, columns), f32),
                pltpu.VMEM((2, 1, count), f32),
                pltpu.VMEM((width, 1, 128), f32),
                pltpu.VMEM((lines + total_lines, 1, 128), f32),
                pltpu.VMEM((n, lines, 1, 128), f32),
                pltpu.VMEM((group + 1, max(8, RAW), half), f32),
                dma((SPLIT + 1, held // LOAD)),
                dma((1,)),
                dma((1,)),
                dma((SPLIT + 1,)),
                dma((1,)),
                dma((1,)),
                dma((1,)),
                dma((1,)),
                dma((4,)),
                dma((4,)),
                dma((max(1, group - 1), 5)),
                dma((max(1, group - 1), 5)),
                dma((layers, k_count - 2)),
                dma((n, 2)),
                dma((group + 1,)),
                dma((group + 1,)),
            ],
            compiler_params=pltpu.CompilerParams(
                collective_id=0, has_side_effects=True, vmem_limit_bytes=VMEM_LIMIT
            ),
            name="gather",
        )(*(pltpu.with_memory_space_constraint(a, pltpu.HBM) for a in arrays))
        gate, up, whole_gate, whole_up, scale_gate, scale_up, serve = pl.pallas_call(
            finish_kernel,
            out_shape=(
                jax.ShapeDtypeStruct((n, held, columns), bf16),
                jax.ShapeDtypeStruct((n, held, columns), bf16),
                jax.ShapeDtypeStruct((held, columns), f32),
                jax.ShapeDtypeStruct((held, columns), f32),
                jax.ShapeDtypeStruct((1, columns), f32),
                jax.ShapeDtypeStruct((1, columns), f32),
                jax.ShapeDtypeStruct((total_lines, 128), bf16),
            ),
            in_specs=[any_space] * 4,
            out_specs=(hbm_space,) * 7,
            scratch_shapes=[dma((7,))],
            compiler_params=pltpu.CompilerParams(vmem_limit_bytes=1 << 20),
            cost_estimate=pl.CostEstimate(flops=FLOPS, bytes_accessed=0, transcendentals=0),
            name="finish",
        )(*results[:4])
        if hidden:
            inner = [(group, 0), ((layers - 2) * group, (layers - 1) * group)]
            ring = [(a + i, b + i) for a, b in inner for i in range(group)]
            swap = [(i, i + 1 - 2 * (i % 2)) for i in range(n)]
            far = lax.ppermute(results[4], "shard", ring)
            near = lax.ppermute(results[5], "shard", swap)
            up = pl.pallas_call(
                functools.partial(patch_kernel, layers, group, stop - held),
                out_shape=jax.ShapeDtypeStruct((n, held, columns), bf16),
                in_specs=[any_space] * 3,
                out_specs=any_space,
                scratch_shapes=[dma((3,))],
                input_output_aliases={2: 0},
                compiler_params=pltpu.CompilerParams(vmem_limit_bytes=1 << 20),
                name="patch",
            )(far, near, up)
        return (
            gate.reshape(-1, columns), up.reshape(-1, columns), scale_gate.reshape(-1), scale_up.reshape(-1),
            serve.reshape(-1), whole_gate, whole_up,
        )

    return jax.shard_map(
        body,
        mesh=mesh,
        in_specs=(P("shard", "width"),) * 6 + (P(("shard", "width")),) * 2,
        out_specs=(
            P(None, "width"),
            P(None, "width"),
            P("width"),
            P("width"),
            P(),
            P("shard", "width"),
            P("shard", "width"),
        ),
        check_vma=False,
    )
```

time: 178 us -> 174 us (0.978)
  Pallas kernels: 178 us -> 171 us
  starting transfers between devices: 0 us -> 2.04 us
    pallas_call x1, Pallas kernels: 170 us -> 163 us  [body(): pl.pallas_call(functools.partial(gather_kernel, n, width, layers, group,...]
    ppermute x0 -> x2, starting transfers between devices: none -> 2.04 us  [the longest x1 1.29 us: body(): far = lax.ppermute(results[4], 'shard', ring)]
  transfers between devices with their start and end apart: 0 -> 2, of which waited for: 0 -> 1; matrix products, arithmetic and copies ran while one was open for 0% -> 0% of each run, Pallas kernels for 0% -> 4%
where the time goes in v3:
time: 174 us
  Pallas kernels  171 us (98%)
  starting transfers between devices  2.04 us (1%)
    pallas_call x1, Pallas kernels, body(): pl.pallas_call(functools.partial(gather_kernel, n, width, layers, group,...  163 us
    pallas_call x1, Pallas kernels, body(): pl.pallas_call(finish_kernel, out_shape=(jax.ShapeDtypeStruct((n, held, c...  7.3 us
  transfers between devices with their start and end apart: 2, of which 1 were waited for; matrix products, arithmetic and copies ran while one was open for 0% of the time, Pallas kernels for 4%

profile of v3, /device:TPU:0, one launch (start us, length us, event | category | flops | bytes accessed | tf_op | source)
XLA Modules:
  0.0 173.9 jit_solution(8295962860803519311)
XLA Ops:
  0.6 162.8 %gather.1 = (bf16[8,512,2048]{2,1,0:T(8,128)(2,1)S(1)}, f32[512,2048]{1,0:T(8,128)S(1)}, f32[2,1,2048]{2,1,0:T(1,128)S(1)}, bf16[16,128]{1,0:T(8,128)(2,1)S(1)},...) custom-call(f32[256,2048]{1,0:T(8,128)} %wg.1, f32[256,2048]{1,0:T(8,128)} %mg.1, f32[256,2048]{1,0:T(8,128)} %sg.1, ...), custom_call_target="tpu_custom_call" | custom-call | tf_op jit(solution)/shard_map/gather/pallas_call | solution.py:476
  163.4 1.3 collective-permute-start
  164.7 0.8 collective-permute-start.1
  165.5 7.3 %finish.1 = (bf16[8,256,2048]{2,1,0:T(8,128)(2,1)}, bf16[8,256,2048]{2,1,0:T(8,128)(2,1)}, f32[256,2048]{1,0:T(8,128)}, f32[256,2048]{1,0:T(8,128)}, f32[1,2048]...) custom-call(bf16[8,512,2048]{2,1,0:T(8,128)(2,1)S(1)} %get-tuple-element.20.out, ...), custom_call_target="tpu_custom_call" | custom-call | flops 100000000 | tf_op jit(solution)/shard_map/finish/pallas_call | solution.py:523
  172.8 0.0 collective-permute-done.1.near
  172.8 0.3 collective-permute-done.far
  173.0 0.8 patch.1
Async XLA Ops:
  163.4 9.6 %collective-permute-start = (bf16[80,2048]{1,0:T(8,128)(2,1)S(1)}, bf16[80,2048]{1,0:T(8,128)(2,1)S(1)}, u32[]{:S(2)}, u32[]{:S(2)}) collective-permute-start(bf16[80,2048]{1,0:T(8,128)(2,1)S(1)} %get-tuple-element.25), channel_id=1, source_target_pairs={{8,0},{12,4},{16,24},{20,28},{9,1},{13,5},{17,25},{21,29},{10,2},{... | collective-permute-start | bytes 983048 | tf_op jit(solution)/shard_map/ppermute | solution.py:545
  164.7 8.1 %collective-permute-start.1 = (bf16[64,2048]{1,0:T(8,128)(2,1)S(1)}, bf16[64,2048]{1,0:T(8,128)(2,1)S(1)}, u32[]{:S(2)}, u32[]{:S(2)}) collective-permute-start(bf16[64,2048]{1,0:T(8,128)(2,1)S(1)} %get-tuple-element.26), channel_id=1, source_target_pairs={{0,4},{4,0},{8,12},{12,8},{16,20},{20,16},{24,28},{28,24},{1,5},{5... | collective-permute-start | bytes 786440 | tf_op jit(solution)/shard_map/ppermute | solution.py:546

commit v4 on v3

--- a/solution.py
+++ b/solution.py
@@ -25,12 +25,16 @@
 FLOPS = 100_000_000
 
 
+def load_rows(held):
+    return [min(SPLIT * LOAD, held)] * SPLIT + [min(2 * LOAD, held // 2)]
+
+
 def gather_kernel(
     n, width, layers, group, chunks, hidden, count,
     wg, mg, sg, wu, mu, su, train, change,
     out, whole, scale_ref, norm, ends, sides,
-    moment, square, mx, maxbuf, inv, terms, pieces, share, shares, land,
-    in_sem, term_sem, ms, mr, ns1, nr1, ns2, nr2, us, ds, ys, yr, zr, zl, es, er,
+    moment, square, mx, maxbuf, inv, linemax, terms, pieces, share, shares, land,
+    in_sem, term_sem, ms, mr, ls, cs, mc, ns1, nr1, ns2, nr2, us, ds, ys, yr, zr, zl, es, er,
 ):
     s, w = lax.axis_index("shard"), lax.axis_index("width")
     z, g = s // group, lax.rem(s, group)
@@ -40,11 +44,12 @@
     half = columns // SPLIT
     trios = ((wg, whole), (mg, moment), (sg, square)), ((wu, whole), (mu, moment), (su, square))
     phases = [(0, i * half, half) for i in range(SPLIT)] + [(1, 0, columns)]
+    block_rows = load_rows(held)
 
     def load(p, i, c):
         m, left, size = phases[p]
         source, target = trios[m][i]
-        rows = LOAD * columns // size
+        rows = block_rows[p]
         at = pl.multiple_of(c * rows, rows)
         cols = pl.ds(left, size)
         return pltpu.make_async_copy(
@@ -52,7 +57,13 @@
         )
 
     def loads(p):
-        return held * phases[p][2] // (LOAD * columns)
+        return held // block_rows[p]
+
+    barrier = pltpu.get_barrier_semaphore()
+    for j in range(1, n):
+        pl.semaphore_signal(barrier, inc=1, device_id=(lax.rem(s + j, n), w), device_id_type=MESH)
+    for j in range(1, width):
+        pl.semaphore_signal(barrier, inc=1, device_id=(s, lax.rem(w + j, width)), device_id_type=MESH)
 
     for i, ref in enumerate((train, change)):
         pltpu.make_async_copy(ref, terms.at[i], term_sem.at[0]).start()
@@ -62,12 +73,6 @@
             for i in range(3):
                 load(p, i, c).start()
 
-    barrier = pltpu.get_barrier_semaphore()
-    for j in range(1, n):
-        pl.semaphore_signal(barrier, inc=1, device_id=(lax.rem(s + j, n), w), device_id_type=MESH)
-    for j in range(1, width):
-        pl.semaphore_signal(barrier, inc=1, device_id=(s, lax.rem(w + j, width)), device_id_type=MESH)
-
     def max_copy(p, j):
         m, left, size = phases[p]
         cols = pl.ds(left, size)
@@ -80,6 +85,34 @@
         for j in range(1, n):
             max_copy(p, j).start()
 
+    def line_peer(d):
+        return lax.rem(z + d, layers) * group + g
+
+    def line_send(p):
+        m, left, size = phases[p]
+        cols = pl.ds(left, size)
+        for d in range(1, layers):
+            pltpu.make_async_remote_copy(
+                mx.at[m, :, cols], maxbuf.at[m, s, :, cols], ls.at[m], mr.at[p],
+                device_id=(line_peer(d), w), device_id_type=MESH,
+            ).start()
+
+    def combine(p):
+        m, left, size = phases[p]
+        cols = pl.ds(left, size)
+        top = mx[m, :, cols]
+        if layers > 1:
+            others = maxbuf.at[m, pl.ds(0, layers - 1), :, cols]
+            pltpu.make_async_copy(others, others, mr.at[p]).wait()
+            for d in range(1, layers):
+                top = jnp.maximum(top, maxbuf[m, line_peer(d), :, cols])
+        linemax[m, g, :, cols] = top
+        for j in range(1, group):
+            pltpu.make_async_remote_copy(
+                linemax.at[m, g, :, cols], linemax.at[m, g, :, cols], cs.at[m], mc.at[p - 1],
+                device_id=(partner(j), w), device_id_type=MESH,
+            ).start()
+
     def partner(j):
         return z * group + lax.rem(g + j, group)
 
@@ -102,12 +135,11 @@
             device_id=(lax.rem(s + j, n), w), device_id_type=MESH,
         )
 
-    trio = moment.at[pl.ds(0, 3 * LOAD)]
-
     def update(p):
         m, left, size = phases[p]
         cols = pl.ds(left, size)
-        rows = LOAD * columns // size
+        rows = block_rows[p]
+        trio = moment.at[pl.ds(0, 3 * rows * size // columns)]
 
         def chunk(c, top):
             pltpu.make_async_copy(trio, trio, in_sem.at[p, c]).wait()
@@ -127,11 +159,18 @@
     def scale(p):
         m, left, size = phases[p]
         cols = pl.ds(left, size)
-        others = maxbuf.at[m, pl.ds(0, n - 1), :, cols]
-        pltpu.make_async_copy(others, others, mr.at[p]).wait()
-        top = mx[m, :, cols]
-        for j in range(1, n):
-            top = jnp.maximum(top, maxbuf[m, lax.rem(s + n - j, n), :, cols])
+        if p:
+            others = linemax.at[m, pl.ds(0, group - 1), :, cols]
+            pltpu.make_async_copy(others, others, mc.at[p - 1]).wait()
+            top = linemax[m, 0, :, cols]
+            for j in range(1, group):
+                top = jnp.maximum(top, linemax[m, j, :, cols])
+        else:
+            others = maxbuf.at[m, pl.ds(0, n - 1), :, cols]
+            pltpu.make_async_copy(others, others, mr.at[p]).wait()
+            top = mx[m, :, cols]
+            for j in range(1, n):
+                top = jnp.maximum(top, maxbuf[m, lax.rem(s + n - j, n), :, cols])
         scale_ref[m, :, cols] = top
         inv[m, :, cols] = 1.0 / top
 
@@ -141,11 +180,11 @@
 
     def raw_all(act):
         if raw:
-            @pl.when(z + 1 < layers)
+            @pl.when(z + 2 == layers)
             def _():
                 act(raw_copy(0))
 
-            @pl.when(z > 0)
+            @pl.when(z == 1)
             def _():
                 act(raw_copy(1))
 
@@ -153,9 +192,9 @@
                 act(raw_copy(1 + j))
 
     raw_all(lambda c: c.start())
-    for p in range(1, SPLIT):
+    for p in range(1, SPLIT + 1):
         update(p)
-        max_send(p)
+        line_send(p)
     lane = lax.broadcasted_iota(jnp.int32, (1, 128), 1)
     per = 128 // count
     spot = lax.rem(s * width + w, per)
@@ -181,14 +220,14 @@
             place(source, k), place(source, k), send, recv, device_id=(device, w), device_id_type=MESH
         )
 
-    def landed(source, k):
-        return zl.at[source, k - late] if k >= late else zr.at[source // group, k]
+    def landed(source, k, shift):
+        return zl.at[source, k - late] if k >= late else zr.at[source // group - shift, k]
 
     def up(source, k):
-        return copy(source, k, us.at[kind(k)], landed(source, k), above)
+        return copy(source, k, us.at[kind(k)], landed(source, k, 0), above)
 
     def down(source, k):
-        return copy(source, k, ds.at[kind(k)], landed(source, k), below)
+        return copy(source, k, ds.at[kind(k)], landed(source, k, 1), below)
 
     def across(source, k, j):
         spot = 4 if k == side else kind(k)
@@ -199,8 +238,8 @@
         for j in range(1, group):
             across(source, k, j).start()
 
-    def arrived(source, k):
-        pltpu.make_async_copy(place(source, k), place(source, k), landed(source, k)).wait()
+    def arrived(source, k, shift=0):
+        pltpu.make_async_copy(place(source, k), place(source, k), landed(source, k, shift)).wait()
 
     def settle(sem, many, size):
         block = out.at[pl.ds(0, many), pl.ds(0, size)]
@@ -231,12 +270,22 @@
     for k in range(1, late):
         start, size, left, wide = chunks[k]
         if start < held:
-            scale(left // half)
-            divide(0, held, left, wide)
+            if k == 1 or start == 0:
+                scale(left // half)
+                divide(0, held, left, wide)
             send(k)
             if k == 1:
-                update(SPLIT)
-                max_send(SPLIT)
+                for p in range(1, SPLIT + 1):
+                    combine(p)
+                if raw:
+                    @pl.when(z + 2 < layers)
+                    def _():
+                        up(s, 0).start()
+
+                    @pl.when(z > 1)
+                    def _():
+                        down(s, 0).start()
+
         else:
             if done == held:
                 scale(SPLIT)
@@ -270,12 +319,24 @@
         cols = pl.ds(0, half)
         out[source, pl.ds(0, raw), cols] = (land[lane] * inv[0, :, cols]).astype(out.dtype)
 
+    def receive(d, k, source, lane, end):
+        if d == 1 and k == 0:
+            @pl.when(end)
+            def _():
+                take(lane, source)
+
+            @pl.when(jnp.logical_not(end))
+            def _():
+                arrived(source, k, lane)
+        else:
+            arrived(source, k, lane)
+
     for d in range(1, layers):
         for k in range(0 if raw else 1, late):
             @pl.when(z - d >= 0)
             def _():
                 source = s - d * group
-                take(0, source) if d == 1 and k == 0 else arrived(source, k)
+                receive(d, k, source, 0, z + 1 == layers)
 
                 @pl.when(z + 1 < layers)
                 def _():
@@ -286,7 +347,7 @@
             @pl.when(z + d < layers)
             def _():
                 source = s + d * group
-                take(1, source) if d == 1 and k == 0 else arrived(source, k)
+                receive(d, k, source, 1, z == 0)
 
                 @pl.when(z > 0)
                 def _():
@@ -362,8 +423,9 @@
         def _():
             for sems, more, many in ((us, layers - 1 - level, level), (ds, level, layers - 1 - level)):
                 if more:
-                    if many and raw:
-                        settle(sems.at[0], many, raw_lines)
+                    own = 1 if more > 1 else 0
+                    if many + own and raw:
+                        settle(sems.at[0], many + own, raw_lines)
                     settle(sems.at[1], many + 1, early - raw_lines)
                     for k in lates:
                         own = 0 if k == tail and more == 1 else 1
@@ -386,8 +448,17 @@
         share[lines + r] = row
     norm[...] = share[pl.ds(lines, total_lines), 0, :].astype(norm.dtype)
     pltpu.make_async_copy(others, others, ns2.at[0]).wait()
-    block = maxbuf.at[:, pl.ds(0, n - 1)]
+    block = maxbuf.at[0, pl.ds(0, n - 1), :, pl.ds(0, half)]
     pltpu.make_async_copy(block, block, ms.at[0]).wait()
+    if layers > 1:
+        for m, size in ((0, columns - half), (1, columns)):
+            if size:
+                block = maxbuf.at[m, pl.ds(0, layers - 1), :, pl.ds(0, size)]
+                pltpu.make_async_copy(block, block, ls.at[m]).wait()
+    for m, size in ((0, columns - half), (1, columns)):
+        if size:
+            block = linemax.at[m, pl.ds(0, group - 1), :, pl.ds(0, size)]
+            pltpu.make_async_copy(block, block, cs.at[m]).wait()
     block = pieces.at[pl.ds(0, width - 1)]
     pltpu.make_async_copy(block, block, ns1.at[0]).wait()
 
@@ -456,7 +527,7 @@
         early = 2 * held - late
         ends = min(ENDS, late // (2 * TILE) * TILE)
         half = columns // SPLIT
-        chunks = [(0, RAW, 0, half), (RAW, held - RAW, 0, half)]
+        chunks = [(0, RAW, 0, half), (RAW, held // 2 - RAW, 0, half), (held // 2, held - held // 2, 0, half)]
         chunks += [(0, held, i * half, half) for i in range(1, SPLIT)]
         stop = early - SIDES if hidden else early
         cuts = [held + (stop - held) * i // (PARTS * TILE) * TILE for i in range(PARTS)] + [stop]
@@ -493,15 +564,19 @@
                 pltpu.VMEM((2, 1, columns), f32),
                 pltpu.VMEM((2, n, 1, columns), f32),
                 pltpu.VMEM((2, 1, columns), f32),
+                pltpu.VMEM((2, group, 1, columns), f32),
                 pltpu.VMEM((2, 1, count), f32),
                 pltpu.VMEM((width, 1, 128), f32),
                 pltpu.VMEM((lines + total_lines, 1, 128), f32),
                 pltpu.VMEM((n, lines, 1, 128), f32),
                 pltpu.VMEM((group + 1, max(8, RAW), half), f32),
-                dma((SPLIT + 1, held // LOAD)),
+                dma((SPLIT + 1, held // min(load_rows(held)))),
                 dma((1,)),
                 dma((1,)),
                 dma((SPLIT + 1,)),
+                dma((2,)),
+                dma((2,)),
+                dma((SPLIT,)),
                 dma((1,)),
                 dma((1,)),
                 dma((1,)),
@@ -510,7 +585,7 @@
                 dma((4,)),
                 dma((max(1, group - 1), 5)),
                 dma((max(1, group - 1), 5)),
-                dma((layers, k_count - 2)),
+                dma((max(1, layers - 1), k_count - 2)),
                 dma((n, 2)),
                 dma((group + 1,)),
                 dma((group + 1,)),

time: 174 us -> 173 us (level)
  transfers between devices with their start and end apart: 2 -> 2, of which waited for: 1 -> 0; matrix products, arithmetic and copies ran while one was open for 0% -> 0% of each run, Pallas kernels for 4% -> 4%
where the time goes in v4:
time: 173 us
  Pallas kernels  170 us (98%)
  starting transfers between devices  2.31 us (1%)
    pallas_call x1, Pallas kernels, body(): pl.pallas_call(functools.partial(gather_kernel, n, width, layers, group,...  162 us
    pallas_call x1, Pallas kernels, body(): pl.pallas_call(finish_kernel, out_shape=(jax.ShapeDtypeStruct((n, held, c...  7.3 us
  transfers between devices with their start and end apart: 2, of which 0 were waited for; matrix products, arithmetic and copies ran while one was open for 0% of the time, Pallas kernels for 4%

profile of v4, /device:TPU:0, one launch (start us, length us, event | category | flops | bytes accessed | tf_op | source)
XLA Modules:
  0.0 172.9 jit_solution(9568173602592715036)
XLA Ops:
  0.6 161.7 %gather.1 = (bf16[8,512,2048]{2,1,0:T(8,128)(2,1)S(1)}, f32[512,2048]{1,0:T(8,128)S(1)}, f32[2,1,2048]{2,1,0:T(1,128)S(1)}, bf16[16,128]{1,0:T(8,128)(2,1)S(1)},...) custom-call(f32[256,2048]{1,0:T(8,128)} %wg.1, f32[256,2048]{1,0:T(8,128)} %mg.1, f32[256,2048]{1,0:T(8,128)} %sg.1, ...), custom_call_target="tpu_custom_call" | custom-call | tf_op jit(solution)/shard_map/gather/pallas_call | solution.py:547
  162.4 1.3 collective-permute-start
  163.7 1.0 collective-permute-start.1
  164.7 7.3 %finish.1 = (bf16[8,256,2048]{2,1,0:T(8,128)(2,1)}, bf16[8,256,2048]{2,1,0:T(8,128)(2,1)}, f32[256,2048]{1,0:T(8,128)}, f32[256,2048]{1,0:T(8,128)}, f32[1,2048]...) custom-call(bf16[8,512,2048]{2,1,0:T(8,128)(2,1)S(1)} %get-tuple-element.20.out, ...), custom_call_target="tpu_custom_call" | custom-call | flops 100000000 | tf_op jit(solution)/shard_map/finish/pallas_call | solution.py:598
  172.0 0.0 collective-permute-done.1.near
  172.0 0.0 collective-permute-done.far
  172.1 0.8 patch.1
Async XLA Ops:
  162.4 9.7 %collective-permute-start = (bf16[80,2048]{1,0:T(8,128)(2,1)S(1)}, bf16[80,2048]{1,0:T(8,128)(2,1)S(1)}, u32[]{:S(2)}, u32[]{:S(2)}) collective-permute-start(bf16[80,2048]{1,0:T(8,128)(2,1)S(1)} %get-tuple-element.25), channel_id=1, source_target_pairs={{8,0},{12,4},{16,24},{20,28},{9,1},{13,5},{17,25},{21,29},{10,2},{... | collective-permute-start | bytes 983048 | tf_op jit(solution)/shard_map/ppermute | solution.py:620
  163.7 8.3 %collective-permute-start.1 = (bf16[64,2048]{1,0:T(8,128)(2,1)S(1)}, bf16[64,2048]{1,0:T(8,128)(2,1)S(1)}, u32[]{:S(2)}, u32[]{:S(2)}) collective-permute-start(bf16[64,2048]{1,0:T(8,128)(2,1)S(1)} %get-tuple-element.26), channel_id=1, source_target_pairs={{0,4},{4,0},{8,12},{12,8},{16,20},{20,16},{24,28},{28,24},{1,5},{5... | collective-permute-start | bytes 786440 | tf_op jit(solution)/shard_map/ppermute | solution.py:621

commit v5 on v4

--- a/solution.py
+++ b/solution.py
@@ -15,8 +15,8 @@
 UNIT = 16
 TILE = 8
 RAW = 32
-ENDS = 40
-SIDES = 64
+ENDS = 56
+SIDES = 96
 PARTS = 2
 SPLIT = 2
 LOAD = 32
@@ -40,6 +40,8 @@
     z, g = s // group, lax.rem(s, group)
     above, below = lax.rem(s + group, n), lax.rem(s + n - group, n)
     raw = chunks[0][1]
+    lead = lax.rem(w, 2) == 1
+    rest = lax.rem(w, 2) == 0
     held, columns = wg.shape
     half = columns // SPLIT
     trios = ((wg, whole), (mg, moment), (sg, square)), ((wu, whole), (mu, moment), (su, square))
@@ -273,10 +275,19 @@
             if k == 1 or start == 0:
                 scale(left // half)
                 divide(0, held, left, wide)
+            if k == 1:
+                @pl.when(rest)
+                def _():
+                    for p in range(1, SPLIT + 1):
+                        combine(p)
+
             send(k)
             if k == 1:
-                for p in range(1, SPLIT + 1):
-                    combine(p)
+                @pl.when(lead)
+                def _():
+                    for p in range(1, SPLIT + 1):
+                        combine(p)
+
                 if raw:
                     @pl.when(z + 2 < layers)
                     def _():
@@ -525,7 +536,7 @@
         hidden = layers > 2 and group == 2
         late = -(-held // (3 * TILE)) * TILE
         early = 2 * held - late
-        ends = min(ENDS, late // (2 * TILE) * TILE)
+        ends = min(ENDS, late - TILE)
         half = columns // SPLIT
         chunks = [(0, RAW, 0, half), (RAW, held // 2 - RAW, 0, half), (held // 2, held - held // 2, 0, half)]
         chunks += [(0, held, i * half, half) for i in range(1, SPLIT)]

time: 173 us -> 171 us (0.988)
  Pallas kernels: 170 us -> 167 us
    pallas_call x1, Pallas kernels: 162 us -> 159 us  [body(): pl.pallas_call(functools.partial(gather_kernel, n, width, layers, group,...]
  transfers between devices with their start and end apart: 2 -> 2, of which waited for: 0 -> 1; matrix products, arithmetic and copies ran while one was open for 0% -> 0% of each run, Pallas kernels for 4% -> 4%
where the time goes in v5:
time: 171 us
  Pallas kernels  167 us (98%)
  starting transfers between devices  2.16 us (1%)
    pallas_call x1, Pallas kernels, body(): pl.pallas_call(functools.partial(gather_kernel, n, width, layers, group,...  159 us
    pallas_call x1, Pallas kernels, body(): pl.pallas_call(finish_kernel, out_shape=(jax.ShapeDtypeStruct((n, held, c...  7.3 us
  transfers between devices with their start and end apart: 2, of which 1 were waited for; matrix products, arithmetic and copies ran while one was open for 0% of the time, Pallas kernels for 4%

profile of v5, /device:TPU:0, one launch (start us, length us, event | category | flops | bytes accessed | tf_op | source)
XLA Modules:
  0.0 171.3 jit_solution(14988375590463737885)
XLA Ops:
  0.6 159.1 %gather.1 = (bf16[8,512,2048]{2,1,0:T(8,128)(2,1)S(1)}, f32[512,2048]{1,0:T(8,128)S(1)}, f32[2,1,2048]{2,1,0:T(1,128)S(1)}, bf16[16,128]{1,0:T(8,128)(2,1)S(1)},...) custom-call(f32[256,2048]{1,0:T(8,128)} %wg.1, f32[256,2048]{1,0:T(8,128)} %mg.1, f32[256,2048]{1,0:T(8,128)} %sg.1, ...), custom_call_target="tpu_custom_call" | custom-call | tf_op jit(solution)/shard_map/gather/pallas_call | solution.py:558
  159.7 1.3 collective-permute-start
  161.0 0.9 collective-permute-start.1
  161.9 7.3 %finish.1 = (bf16[8,256,2048]{2,1,0:T(8,128)(2,1)}, bf16[8,256,2048]{2,1,0:T(8,128)(2,1)}, f32[256,2048]{1,0:T(8,128)}, f32[256,2048]{1,0:T(8,128)}, f32[1,2048]...) custom-call(bf16[8,512,2048]{2,1,0:T(8,128)(2,1)S(1)} %get-tuple-element.20.out, ...), custom_call_target="tpu_custom_call" | custom-call | flops 100000000 | tf_op jit(solution)/shard_map/finish/pallas_call | solution.py:609
  169.2 0.0 collective-permute-done.1.near
  169.2 1.1 collective-permute-done.far
  170.3 0.9 patch.1
Async XLA Ops:
  159.7 10.6 %collective-permute-start = (bf16[112,2048]{1,0:T(8,128)(2,1)S(1)}, bf16[112,2048]{1,0:T(8,128)(2,1)S(1)}, u32[]{:S(2)}, u32[]{:S(2)}) collective-permute-start(bf16[112,2048]{1,0:T(8,128)(2,1)S(1)} %get-tuple-element.25), channel_id=1, source_target_pairs={{8,0},{12,4},{16,24},{20,28},{9,1},{13,5},{17,25},{21,29},{10,2},{... | collective-permute-start | bytes 1376264 | tf_op jit(solution)/shard_map/ppermute | solution.py:631
  161.0 8.2 %collective-permute-start.1 = (bf16[96,2048]{1,0:T(8,128)(2,1)S(1)}, bf16[96,2048]{1,0:T(8,128)(2,1)S(1)}, u32[]{:S(2)}, u32[]{:S(2)}) collective-permute-start(bf16[96,2048]{1,0:T(8,128)(2,1)S(1)} %get-tuple-element.26), channel_id=1, source_target_pairs={{0,4},{4,0},{8,12},{12,8},{16,20},{20,16},{24,28},{28,24},{1,5},{5... | collective-permute-start | bytes 1179656 | tf_op jit(solution)/shard_map/ppermute | solution.py:632

commit v6 on v5

--- a/solution.py
+++ b/solution.py
@@ -16,7 +16,7 @@
 TILE = 8
 RAW = 32
 ENDS = 56
-SIDES = 96
+SIDES = 104
 PARTS = 2
 SPLIT = 2
 LOAD = 32

time: 171 us -> 171 us (level)
  transfers between devices with their start and end apart: 2 -> 2, of which waited for: 1 -> 2; matrix products, arithmetic and copies ran while one was open for 0% -> 0% of each run, Pallas kernels for 4% -> 4%
where the time goes in v6:
time: 171 us
  Pallas kernels  167 us (98%)
  starting transfers between devices  2.04 us (1%)
    pallas_call x1, Pallas kernels, body(): pl.pallas_call(functools.partial(gather_kernel, n, width, layers, group,...  159 us
    pallas_call x1, Pallas kernels, body(): pl.pallas_call(finish_kernel, out_shape=(jax.ShapeDtypeStruct((n, held, c...  7.3 us
  transfers between devices with their start and end apart: 2, of which 2 were waited for; matrix products, arithmetic and copies ran while one was open for 0% of the time, Pallas kernels for 4%

profile of v6, /device:TPU:0, one launch (start us, length us, event | category | flops | bytes accessed | tf_op | source)
XLA Modules:
  0.0 170.9 jit_solution(13994143465602917496)
XLA Ops:
  0.6 158.9 %gather.1 = (bf16[8,512,2048]{2,1,0:T(8,128)(2,1)S(1)}, f32[512,2048]{1,0:T(8,128)S(1)}, f32[2,1,2048]{2,1,0:T(1,128)S(1)}, bf16[16,128]{1,0:T(8,128)(2,1)S(1)},...) custom-call(f32[256,2048]{1,0:T(8,128)} %wg.1, f32[256,2048]{1,0:T(8,128)} %mg.1, f32[256,2048]{1,0:T(8,128)} %sg.1, ...), custom_call_target="tpu_custom_call" | custom-call | tf_op jit(solution)/shard_map/gather/pallas_call | solution.py:558
  159.6 1.3 collective-permute-start
  160.9 0.7 collective-permute-start.1
  161.6 7.3 %finish.1 = (bf16[8,256,2048]{2,1,0:T(8,128)(2,1)}, bf16[8,256,2048]{2,1,0:T(8,128)(2,1)}, f32[256,2048]{1,0:T(8,128)}, f32[256,2048]{1,0:T(8,128)}, f32[1,2048]...) custom-call(bf16[8,512,2048]{2,1,0:T(8,128)(2,1)S(1)} %get-tuple-element.20.out, ...), custom_call_target="tpu_custom_call" | custom-call | flops 100000000 | tf_op jit(solution)/shard_map/finish/pallas_call | solution.py:609
  168.9 0.1 collective-permute-done.1.near
  169.1 0.9 collective-permute-done.far
  169.9 0.9 patch.1
Async XLA Ops:
  159.6 10.4 %collective-permute-start = (bf16[112,2048]{1,0:T(8,128)(2,1)S(1)}, bf16[112,2048]{1,0:T(8,128)(2,1)S(1)}, u32[]{:S(2)}, u32[]{:S(2)}) collective-permute-start(bf16[112,2048]{1,0:T(8,128)(2,1)S(1)} %get-tuple-element.25), channel_id=1, source_target_pairs={{8,0},{12,4},{16,24},{20,28},{9,1},{13,5},{17,25},{21,29},{10,2},{... | collective-permute-start | bytes 1376264 | tf_op jit(solution)/shard_map/ppermute | solution.py:631
  160.9 8.2 %collective-permute-start.1 = (bf16[104,2048]{1,0:T(8,128)(2,1)S(1)}, bf16[104,2048]{1,0:T(8,128)(2,1)S(1)}, u32[]{:S(2)}, u32[]{:S(2)}) collective-permute-start(bf16[104,2048]{1,0:T(8,128)(2,1)S(1)} %get-tuple-element.26), channel_id=1, source_target_pairs={{0,4},{4,0},{8,12},{12,8},{16,20},{20,16},{24,28},{28,24},{1,5},{5... | collective-permute-start | bytes 1277960 | tf_op jit(solution)/shard_map/ppermute | solution.py:632
